TPU v7x, 256 devices: a whole 4x4x8 slice. The times are simulated.
256 devices in a mesh: gx: 2 (over x_lo), gy: 8 (over x_hi, y), gz: 16 (over z, core).
Axes of the slice: x: 4 (x_hi: 2, x_lo: 2; x = x_hi * 2 + x_lo), y: 4, z: 8, core: 2. Of those that a mesh axis runs over, the one named last changes fastest.
Arguments:
- volume: bfloat16 [32, 64, 64, 256], P(None, 'gx', 'gy', 'gz'), may hold values from -6 to 6
- weight_a: bfloat16 [3, 3, 3, 32, 64], replicated, may hold values from -0.21875 to 0.21875
- bias_a: float32 [64], replicated, may hold values from -3 to 3
- weight_b: bfloat16 [3, 3, 3, 64, 128], replicated, may hold values from -0.15625 to 0.15625
- bias_b: float32 [128], replicated, may hold values from -3 to 3
- cotangent: bfloat16 [128, 32, 32, 128], P(None, ('gx', 'gz'), 'gy'), may hold values from -24 to 24
Outputs:
- features: bfloat16 [128, 32, 32, 128], P(None, ('gx', 'gz'), 'gy')
- grad_input: bfloat16 [32, 64, 64, 256], P(None, 'gx', 'gy', 'gz')
- grad_weight_a: float32 [3, 3, 3, 32, 64], replicated
- grad_bias_a: float32 [64], replicated
- grad_weight_b: float32 [3, 3, 3, 64, 128], replicated
- grad_bias_b: float32 [128], replicated
All inputs are finite; a program needn't handle non-finite values.
Results may differ from a plain program's by a relative error of at most 0.012.
Values may be sent and summed in bfloat16 or wider, within the bound.
A program may use at most 128 MiB of HBM per device.

v0:
```python
import functools
import math

import jax
import jax.numpy as jnp
from jax import lax
from jax.experimental import pallas as pl
from jax.experimental.pallas import tpu as pltpu
from jax.sharding import PartitionSpec as P

LINE = ("gx", "gz")
MESH = pl.DeviceIdType.MESH


def shared(block, axis, dim, width):
    count = lax.axis_size(axis)
    if count == 1:
        edge = jnp.zeros_like(lax.slice_in_dim(block, 0, width, axis=dim))
        return edge, edge
    forward = [(i, i + 1) for i in range(count - 1)]
    backward = [(target, source) for source, target in forward]
    last = block.shape[dim]
    low = lax.ppermute(lax.slice_in_dim(block, last - width, last, axis=dim), axis, forward)
    high = lax.ppermute(lax.slice_in_dim(block, 0, width, axis=dim), axis, backward)
    return low, high


def widened(flat, planes, rows, depth):
    low, high = shared(flat, LINE, 1, rows * depth)
    if lax.axis_size("gy") == 1:
        gap = jnp.zeros((flat.shape[0], depth), flat.dtype)
        pieces = [gap, low, gap]
        for plane in range(planes):
            pieces += [gap, flat[:, plane * rows * depth : (plane + 1) * rows * depth], gap]
        return jnp.concatenate(pieces + [gap, high, gap], axis=1)
    whole = jnp.concatenate([low, flat, high], axis=1)
    whole = whole.reshape(flat.shape[0], planes + 2, rows, depth)
    low, high = shared(whole, "gy", 2, 1)
    return jnp.concatenate([low, whole, high], axis=2).reshape(flat.shape[0], -1)


def slope_of(value):
    sigma = jax.nn.sigmoid(value)
    return sigma + value * sigma * (1.0 - sigma)


def put_windows(wide_ref, windows, planes, rows, depth):
    wide = wide_ref[...]
    width, extent = wide.shape
    place = lax.broadcasted_iota(jnp.int32, (width, extent), 1) % depth
    loose = wide.astype(jnp.float32)
    before = jnp.where(place == 0, 0.0, pltpu.roll(loose, 1, 1)).astype(jnp.bfloat16)
    after = jnp.where(place == depth - 1, 0.0, pltpu.roll(loose, extent - 1, 1)).astype(jnp.bfloat16)
    size = rows * depth
    for third, moved in enumerate((before, wide, after)):
        for first in range(3):
            for second in range(3):
                at = (first * 9 + second * 3 + third) * width
                for plane in range(planes):
                    begin = ((plane + first) * (rows + 2) + second) * depth
                    windows[at : at + width, plane * size : (plane + 1) * size] = moved[
                        :, begin : begin + size
                    ]


def dot_rows(left, right):
    return lax.dot_general(
        left, right, (((1,), (1,)), ((), ())), preferred_element_type=jnp.float32
    )


def forward_a_kernel(dims, wide_ref, weight_ref, bias_ref, pool_ref, before_ref, pooled_ref, windows):
    planes, rows, depth = dims
    put_windows(wide_ref, windows, *dims)
    before = jnp.dot(weight_ref[...], windows[...], preferred_element_type=jnp.float32)
    before = before + bias_ref[...]
    before_ref[...] = before
    active = before * jax.nn.sigmoid(before)
    size = rows * depth
    for row in range(rows // 2):
        parts = [
            active[:, plane * size + (2 * row + j) * depth : plane * size + (2 * row + j + 1) * depth]
            for plane in range(planes)
            for j in range(2)
        ]
        summed = sum(parts[1:], parts[0])
        paired = jnp.dot(
            summed, pool_ref[...], precision=lax.Precision.HIGHEST, preferred_element_type=jnp.float32
        )
        pooled_ref[:, row * depth // 2 : (row + 1) * depth // 2] = (paired * 0.125).astype(jnp.bfloat16)


def middle_kernel(dims, wide_ref, weight_ref, bias_ref, cot_ref, feat_ref, grad_ref, wb_ref, bb_ref, windows):
    put_windows(wide_ref, windows, *dims)
    before = jnp.dot(weight_ref[...], windows[...], preferred_element_type=jnp.float32)
    before = before + bias_ref[...]
    feat_ref[...] = (before * jax.nn.sigmoid(before)).astype(jnp.bfloat16)
    grad = (cot_ref[...].astype(jnp.float32) * slope_of(before)).astype(jnp.bfloat16)
    grad_ref[...] = grad
    wb_ref[...] = dot_rows(windows[...], grad)
    bb_ref[...] = dot_rows(jnp.ones((8, grad.shape[1]), jnp.bfloat16), grad)


def backward_b_kernel(dims, fine, wide_ref, weight_ref, before_ref, spread_ref, grad_ref, windows):
    put_windows(wide_ref, windows, *dims)
    pooled = jnp.dot(weight_ref[...], windows[...], preferred_element_type=jnp.float32)
    pooled = pooled.astype(jnp.bfloat16)
    planes, rows, depth = fine
    size = rows * depth
    for row in range(rows // 2):
        part = pooled[:, row * depth // 2 : (row + 1) * depth // 2]
        spread = jnp.dot(part, spread_ref[...], preferred_element_type=jnp.float32) * 0.125
        for plane in range(planes):
            for j in range(2):
                begin = plane * size + (2 * row + j) * depth
                slope = slope_of(before_ref[:, begin : begin + depth])
                grad_ref[:, begin : begin + depth] = (spread * slope).astype(jnp.bfloat16)


def weight_a_kernel(dims, wide_ref, grad_ref, wa_ref, ba_ref, windows):
    put_windows(wide_ref, windows, *dims)
    grad = grad_ref[...]
    wa_ref[...] = dot_rows(windows[...], grad)
    ba_ref[...] = dot_rows(jnp.ones((8, grad.shape[1]), jnp.bfloat16), grad)


def backward_a_kernel(dims, wide_ref, weight_ref, out_ref, windows):
    put_windows(wide_ref, windows, *dims)
    out = jnp.dot(weight_ref[...], windows[...], preferred_element_type=jnp.float32)
    out_ref[...] = out.astype(jnp.bfloat16)


def local_kernel(body, outs, windows, flops, *operands):
    moved = sum(x.size * x.dtype.itemsize for x in operands)
    return pl.pallas_call(
        body,
        out_shape=[jax.ShapeDtypeStruct(shape, dtype) for shape, dtype in outs],
        in_specs=[pl.BlockSpec(memory_space=pltpu.VMEM)] * len(operands),
        out_specs=[pl.BlockSpec(memory_space=pltpu.VMEM)] * len(outs),
        scratch_shapes=[pltpu.VMEM(windows, jnp.bfloat16)],
        compiler_params=pltpu.CompilerParams(vmem_limit_bytes=48 * 2**20),
        cost_estimate=pl.CostEstimate(flops=flops, bytes_accessed=moved, transcendentals=0),
    )(*operands)


def partner_of(axis, bit):
    me = lax.axis_index(axis)
    mine = (me // bit) % 2
    return me + bit * (1 - 2 * mine), mine


def sum_kernel(steps, halvings, rows, scales, wa_ref, ba_ref, wb_ref, bb_ref, *rest):
    out_wa, out_ba, out_wb, out_bb, acc, gathered, *scratch = rest
    half, width = wa_ref.shape[0] // 2, wa_ref.shape[1]
    top = wb_ref.shape[0]
    count = len(steps)
    sends = scratch[:count]
    recvs = scratch[count : 2 * count]
    sem_send, sem_recv = scratch[2 * count :]
    partners = [partner_of(axis, bit) for axis, bit in steps]
    barrier = pltpu.get_barrier_semaphore()
    for (axis, _), (partner, _) in zip(steps, partners):
        pl.semaphore_signal(barrier, inc=1, device_id={axis: partner}, device_id_type=MESH)
    acc[:top] = wb_ref[...]
    acc[top : top + half, :width] = wa_ref[:half]
    acc[top : top + half, width:] = wa_ref[half:]
    acc[top + half :] = jnp.zeros((rows - top - half, 128), jnp.float32)
    acc[top + half : top + half + 8, :width] = ba_ref[...]
    acc[top + half + 8 : top + half + 16] = bb_ref[...]
    pl.semaphore_wait(barrier, count)
    offset = 0
    size = rows
    kept = []
    for at, ((axis, _), (partner, mine)) in enumerate(zip(steps, partners)):
        source = acc
        if at < halvings:
            size = size // 2
            away = pl.multiple_of(offset + (1 - mine) * size, 16)
            offset = pl.multiple_of(offset + mine * size, 16)
        else:
            away = offset
        sends[at][...] = source[pl.ds(away, size)].astype(jnp.bfloat16)
        copy = pltpu.make_async_remote_copy(
            src_ref=sends[at],
            dst_ref=recvs[at],
            send_sem=sem_send.at[at],
            recv_sem=sem_recv.at[at],
            device_id={axis: partner},
            device_id_type=MESH,
        )
        copy.start()
        copy.wait()
        if at < halvings:
            acc[pl.ds(offset, size)] = source[pl.ds(offset, size)] + recvs[at][...].astype(jnp.float32)
            kept.append((offset, size))
        else:
            acc[pl.ds(offset, size)] = sends[at][...].astype(jnp.float32) + recvs[at][...].astype(jnp.float32)
    gathered[pl.ds(offset, size)] = acc[pl.ds(offset, size)].astype(jnp.bfloat16)
    for back in range(halvings):
        at = halvings - 1 - back
        begin, extent = kept[at]
        (axis, _), (partner, _) = steps[at], partners[at]
        here = gathered.at[pl.ds(begin, extent)]
        copy = pltpu.make_async_remote_copy(
            src_ref=here,
            dst_ref=here,
            send_sem=sem_send.at[count + back],
            recv_sem=sem_recv.at[count + back],
            device_id={axis: partner},
            device_id_type=MESH,
        )
        copy.start()
        copy.wait()
    scale_a, scale_b = scales
    total = gathered[...].astype(jnp.float32)
    out_wb[...] = total[:top] * scale_b
    out_wa[:half] = total[top : top + half, :width] * scale_a
    out_wa[half:] = total[top : top + half, width:] * scale_a
    out_ba[...] = total[top + half : top + half + 1, :width] * scale_a
    out_bb[...] = total[top + half + 8 : top + half + 9] * scale_b


def summed_grads(wa, ba, wb, bb, scales):
    used = wb.shape[0] + wa.shape[0] // 2 + 16
    rows = used + -used % 128
    cut = {
        axis: [2**i for i in range(lax.axis_size(axis).bit_length() - 1)] for axis in ("gz", "gx", "gy")
    }
    steps = [("gz", bit) for bit in cut["gz"][:1]]
    steps += [("gx", bit) for bit in cut["gx"]] + [("gy", bit) for bit in cut["gy"]]
    steps += [("gz", bit) for bit in cut["gz"][1:]]
    halvings = 0
    sizes = []
    size = rows
    for _ in steps:
        if len(sizes) == halvings and size % 32 == 0:
            size //= 2
            halvings += 1
        sizes.append(size)
    buffers = [pltpu.VMEM((s, 128), jnp.bfloat16) for s in sizes]
    total = len(steps) + halvings
    shapes = [wa.shape, (1, ba.shape[1]), wb.shape, (1, bb.shape[1])]
    return pl.pallas_call(
        functools.partial(sum_kernel, steps, halvings, rows, scales),
        out_shape=[jax.ShapeDtypeStruct(shape, jnp.float32) for shape in shapes],
        in_specs=[pl.BlockSpec(memory_space=pltpu.VMEM)] * 4,
        out_specs=[pl.BlockSpec(memory_space=pltpu.VMEM)] * 4,
        scratch_shapes=[
            pltpu.VMEM((rows, 128), jnp.float32),
            pltpu.VMEM((rows, 128), jnp.bfloat16),
            *buffers,
            *buffers,
            pltpu.SemaphoreType.DMA((total,)),
            pltpu.SemaphoreType.DMA((total,)),
        ],
        compiler_params=pltpu.CompilerParams(collective_id=0, has_side_effects=True),
    )(wa, ba, wb, bb)


def line_ends(axis_sizes):
    across, count = axis_sizes
    total = across * count
    line = lax.axis_index("gx") * count + lax.axis_index("gz")
    after, before = (line + 1) % total, (line + total - 1) % total
    ids = [{"gx": at // count, "gz": at % count} for at in (after, before)]
    return line, total, ids


class Halo:
    def __init__(self, wide, dims, where, sems, at):
        planes, rows, depth = dims
        self.line, self.total, ids = where
        size, stride = rows * depth, (rows + 2) * depth
        spot = lambda plane: wide.at[:, plane * stride + depth : plane * stride + depth + size]
        send, recv = sems
        self.up, self.down = [
            pltpu.make_async_remote_copy(
                src_ref=spot(source),
                dst_ref=spot(target),
                send_sem=send.at[at + i],
                recv_sem=recv.at[at + i],
                device_id=ids[i],
                device_id_type=MESH,
            )
            for i, (source, target) in enumerate(((planes, 0), (1, planes + 1)))
        ]

    def start(self):
        pl.when(self.line < self.total - 1)(self.up.start)
        pl.when(self.line > 0)(self.down.start)

    def wait(self):
        @pl.when(self.line < self.total - 1)
        def _():
            self.up.wait_send()
            self.down.wait_recv()

        @pl.when(self.line > 0)
        def _():
            self.down.wait_send()
            self.up.wait_recv()


class Summing:
    def __init__(self, steps, sizes, acc, gathered, sends, recvs, sems):
        self.steps, self.sizes = steps, sizes
        self.acc, self.gathered, self.sends, self.recvs = acc, gathered, sends, recvs
        self.sems = sems
        self.partners = [partner_of(axis, bit) for axis, bit in steps]
        rows = [acc.shape[0]] + list(sizes)
        self.halvings = sum(a != b for a, b in zip(rows, sizes))
        self.stages = len(steps) + self.halvings
        self.offset = 0
        self.kept = []
        self.flying = None

    def copy(self, stage, source, target, step):
        send, recv = self.sems
        self.flying = pltpu.make_async_remote_copy(
            src_ref=source,
            dst_ref=target,
            send_sem=send.at[stage],
            recv_sem=recv.at[stage],
            device_id={self.steps[step][0]: self.partners[step][0]},
            device_id_type=MESH,
        )
        self.flying.start()

    def start(self, stage):
        if stage < len(self.steps):
            size = self.sizes[stage]
            away = self.offset
            if stage < self.halvings:
                mine = self.partners[stage][1]
                away = pl.multiple_of(self.offset + (1 - mine) * size, 16)
                self.offset = pl.multiple_of(self.offset + mine * size, 16)
                self.kept.append((self.offset, size))
            self.sends[stage][...] = self.acc[pl.ds(away, size)].astype(jnp.bfloat16)
            self.copy(stage, self.sends[stage], self.recvs[stage], stage)
        else:
            step = self.halvings - 1 - (stage - len(self.steps))
            begin, size = self.kept[step]
            here = self.gathered.at[pl.ds(begin, size)]
            self.copy(stage, here, here, step)

    def finish(self, stage):
        self.flying.wait()
        if stage >= len(self.steps):
            return
        here = pl.ds(self.offset, self.sizes[stage])
        came = self.recvs[stage][...].astype(jnp.float32)
        own = self.acc[here] if stage < self.halvings else self.sends[stage][...].astype(jnp.float32)
        total = own + came
        if stage == len(self.steps) - 1:
            self.gathered[here] = total.astype(jnp.bfloat16)
        else:
            self.acc[here] = total


def place(wide, flat, dims):
    planes, rows, depth = dims
    size, stride = rows * depth, (rows + 2) * depth
    for plane in range(planes):
        begin = (plane + 1) * stride + depth
        wide[:, begin : begin + size] = flat[:, plane * size : (plane + 1) * size]


def whole_kernel(setting, *refs):
    fine, coarse, sizes_line, steps, cuts_a, cuts_b, scales = setting
    slab, w_a, b_a, pool, w_b, b_b, cot, v_b, spread, v_a = refs[:10]
    features, grad_slab, out_wa, out_ba, out_wb, out_bb = refs[10:16]
    wide_a, wide_b, wide_gb, wide_ga, win_a, win_b, win_gb, win_ga = refs[16:24]
    before_a, pooled, grad_b, grad_a, acc_a, acc_b, all_a, all_b = refs[24:32]
    count = len(steps)
    send_a, recv_a, send_b, recv_b = [refs[32 + i * count : 32 + (i + 1) * count] for i in range(4)]
    sems = refs[32 + 4 * count :]
    where = line_ends(sizes_line)
    line, total, ids = where
    barrier = pltpu.get_barrier_semaphore()
    for wide in (wide_a, wide_b, wide_gb, wide_ga):
        wide[...] = jnp.zeros_like(wide)
    place(wide_a, slab, fine)
    for axis, bit in steps:
        partner, _ = partner_of(axis, bit)
        pl.semaphore_signal(barrier, inc=1, device_id={axis: partner}, device_id_type=MESH)
    for device in ids:
        pl.semaphore_signal(barrier, inc=1, device_id=device, device_id_type=MESH)
    pl.semaphore_wait(barrier, count + 2)
    halos = [
        Halo(wide, dims, where, sems[:2], 2 * i)
        for i, (wide, dims) in enumerate(
            ((wide_a, fine), (wide_b, coarse), (wide_gb, coarse), (wide_ga, fine))
        )
    ]
    sum_a = Summing(steps, cuts_a, acc_a, all_a, send_a, recv_a, sems[2:4])
    sum_b = Summing(steps, cuts_b, acc_b, all_b, send_b, recv_b, sems[4:6])

    halos[0].start()
    halos[0].wait()
    forward_a_kernel(fine, wide_a, w_a, b_a, pool, before_a, pooled, win_a)
    place(wide_b, pooled, coarse)
    halos[1].start()
    halos[1].wait()
    top_b = out_wb.shape[0]
    middle_kernel(
        coarse, wide_b, w_b, b_b, cot, features, grad_b, acc_b.at[:top_b], acc_b.at[top_b : top_b + 8], win_b
    )
    place(wide_gb, grad_b, coarse)
    halos[2].start()
    acc_b[top_b + 8 :] = jnp.zeros((acc_b.shape[0] - top_b - 8, acc_b.shape[1]), jnp.float32)
    sum_b.start(0)
    halos[2].wait()
    backward_b_kernel(coarse, fine, wide_gb, v_b, before_a, spread, grad_a, win_gb)
    place(wide_ga, grad_a, fine)
    halos[3].start()
    sum_b.finish(0)
    sum_b.start(1)
    grad = grad_a[...]
    half, width = out_wa.shape[0] // 2, out_wa.shape[1]
    acc_a[:half, :width] = dot_rows(win_a[:half], grad)
    acc_a[:half, width:] = dot_rows(win_a[half:], grad)
    acc_a[half:] = jnp.zeros((acc_a.shape[0] - half, acc_a.shape[1]), jnp.float32)
    acc_a[half : half + 8, :width] = dot_rows(jnp.ones((8, grad.shape[1]), jnp.bfloat16), grad)
    sum_b.finish(1)
    sum_b.start(2)
    sum_a.start(0)
    halos[3].wait()
    backward_a_kernel(fine, wide_ga, v_a, grad_slab, win_ga)
    for stage in range(max(sum_a.stages, sum_b.stages - 2)):
        if stage + 2 < sum_b.stages:
            sum_b.finish(stage + 2)
            if stage + 3 < sum_b.stages:
                sum_b.start(stage + 3)
        if stage < sum_a.stages:
            sum_a.finish(stage)
            if stage + 1 < sum_a.stages:
                sum_a.start(stage + 1)
    scale_a, scale_b = scales
    out_wb[...] = all_b[:top_b].astype(jnp.float32) * scale_b
    out_bb[...] = all_b[top_b : top_b + 16].astype(jnp.float32)[:1] * scale_b
    out_wa[:half] = all_a[:half, :width].astype(jnp.float32) * scale_a
    out_wa[half:] = all_a[:half, width:].astype(jnp.float32) * scale_a
    out_ba[...] = all_a[half : half + 16, :width].astype(jnp.float32)[:1] * scale_a


def stage_sizes(rows, steps):
    sizes = []
    for _ in steps:
        halve = rows % 32 == 0 and len(sizes) < 3
        rows = rows // 2 if halve else rows
        sizes.append(rows)
    return sizes


def all_steps():
    cut = {
        axis: [2**i for i in range(lax.axis_size(axis).bit_length() - 1)] for axis in ("gz", "gx", "gy")
    }
    steps = [("gz", bit) for bit in cut["gz"][:1]]
    steps += [("gx", bit) for bit in cut["gx"]] + [("gy", bit) for bit in cut["gy"]]
    return steps + [("gz", bit) for bit in cut["gz"][1:]]


def between_exchanges(fine, coarse, scales, slab, weight_a, bias_a, weight_b, bias_b, cot, pool):
    f32, bf16 = jnp.float32, jnp.bfloat16
    c1, cells = slab.shape
    c2, c3 = weight_b.shape[3:]
    fewer = cells // 8
    steps = all_steps()
    rows_a = 27 * c1 // 2 + 16
    rows_a += -rows_a % 128
    rows_b = 27 * c2 + 16
    rows_b += -rows_b % 128
    cuts_a, cuts_b = stage_sizes(rows_a, steps), stage_sizes(rows_b, steps)
    extent = lambda dims: (dims[0] + 2) * (dims[1] + 2) * dims[2]
    setting = (fine, coarse, (lax.axis_size("gx"), lax.axis_size("gz")), steps, cuts_a, cuts_b, scales)
    buffers = [pltpu.VMEM((n, 128), bf16) for cuts in (cuts_a, cuts_a, cuts_b, cuts_b) for n in cuts]
    outs = [
        ((c3, fewer), bf16),
        ((c1, cells), bf16),
        ((27 * c1, c2), f32),
        ((1, c2), f32),
        ((27 * c2, c3), f32),
        ((1, c3), f32),
    ]
    operands = (
        slab,
        outward(weight_a),
        bias_a[:, None],
        pool,
        outward(weight_b),
        bias_b[:, None],
        cot,
        inward(weight_b),
        pool.T.astype(bf16),
        inward(weight_a),
    )
    most = 2 * len(steps)
    return pl.pallas_call(
        functools.partial(whole_kernel, setting),
        out_shape=[jax.ShapeDtypeStruct(shape, dtype) for shape, dtype in outs],
        in_specs=[pl.BlockSpec(memory_space=pltpu.VMEM)] * len(operands),
        out_specs=[pl.BlockSpec(memory_space=pltpu.VMEM)] * len(outs),
        scratch_shapes=[
            pltpu.VMEM((c1, extent(fine)), bf16),
            pltpu.VMEM((c2, extent(coarse)), bf16),
            pltpu.VMEM((c3, extent(coarse)), bf16),
            pltpu.VMEM((c2, extent(fine)), bf16),
            pltpu.VMEM((27 * c1, cells), bf16),
            pltpu.VMEM((27 * c2, fewer), bf16),
            pltpu.VMEM((27 * c3, fewer), bf16),
            pltpu.VMEM((27 * c2, cells), bf16),
            pltpu.VMEM((c2, cells), f32),
            pltpu.VMEM((c2, fewer), bf16),
            pltpu.VMEM((c3, fewer), bf16),
            pltpu.VMEM((c2, cells), bf16),
            pltpu.VMEM((rows_a, 128), f32),
            pltpu.VMEM((rows_b, 128), f32),
            pltpu.VMEM((rows_a, 128), bf16),
            pltpu.VMEM((rows_b, 128), bf16),
            *buffers,
            pltpu.SemaphoreType.DMA((8,)),
            pltpu.SemaphoreType.DMA((8,)),
            *[pltpu.SemaphoreType.DMA((most,))] * 4,
        ],
        compiler_params=pltpu.CompilerParams(
            collective_id=1, has_side_effects=True, vmem_limit_bytes=60 * 2**20
        ),
    )(*operands)


def outward(weight):
    return weight.reshape(-1, weight.shape[-1]).T


def inward(weight):
    taps = weight[::-1, ::-1, ::-1].reshape(27, *weight.shape[3:])
    return jnp.transpose(taps, (1, 0, 2)).reshape(weight.shape[3], -1)


def on_device(volume, weight_a, bias_a, weight_b, bias_b, cotangent):
    f32, bf16 = jnp.float32, jnp.bfloat16
    count = lax.axis_size("gz")
    devices_all = lax.axis_size("gx") * lax.axis_size("gy") * count
    c1, nx, rows, nz = volume.shape
    cells = nx * rows * nz
    scale_a = 1.0 / math.sqrt(cells * devices_all)
    scale_b = 1.0 / math.sqrt(cells * devices_all // 8)
    c2, c3 = weight_b.shape[3:]
    planes, depth = nx // count, nz * count
    fine = (planes, rows, depth)
    coarse = (planes // 2, rows // 2, depth // 2)
    fewer = cells // 8
    pool = (jnp.arange(depth)[:, None] // 2 == jnp.arange(depth // 2)[None]).astype(f32)
    work_a = 2 * 27 * c1 * c2 * cells
    work_b = 2 * 27 * c2 * c3 * fewer

    slab = lax.all_to_all(volume, "gz", split_axis=1, concat_axis=3, tiled=True).reshape(c1, cells)
    if lax.axis_size("gy") == 1:
        features, grad_slab, sum_wa, sum_ba, sum_wb, sum_bb = between_exchanges(
            fine,
            coarse,
            (scale_a, scale_b),
            slab,
            weight_a,
            bias_a,
            weight_b,
            bias_b,
            cotangent.reshape(c3, fewer),
            pool,
        )
    else:
        wide_a = widened(slab, *fine)
        before_a, pooled = local_kernel(
            functools.partial(forward_a_kernel, fine),
            [((c2, cells), f32), ((c2, fewer), bf16)],
            (27 * c1, cells),
            work_a,
            wide_a,
            outward(weight_a),
            bias_a[:, None],
            pool,
        )
        wide_b = widened(pooled, *coarse)
        features, grad_b, part_wb, part_bb = local_kernel(
            functools.partial(middle_kernel, coarse),
            [((c3, fewer), bf16), ((c3, fewer), bf16), ((27 * c2, c3), f32), ((8, c3), f32)],
            (27 * c2, fewer),
            2 * work_b,
            wide_b,
            outward(weight_b),
            bias_b[:, None],
            cotangent.reshape(c3, fewer),
        )
        (grad_a,) = local_kernel(
            functools.partial(backward_b_kernel, coarse, fine),
            [((c2, cells), bf16)],
            (27 * c3, fewer),
            work_b,
            widened(grad_b, *coarse),
            inward(weight_b),
            before_a,
            pool.T.astype(bf16),
        )
        part_wa, part_ba = local_kernel(
            functools.partial(weight_a_kernel, fine),
            [((27 * c1, c2), f32), ((8, c2), f32)],
            (27 * c1, cells),
            work_a,
            wide_a,
            grad_a,
        )
        (grad_slab,) = local_kernel(
            functools.partial(backward_a_kernel, fine),
            [((c1, cells), bf16)],
            (27 * c2, cells),
            work_a,
            widened(grad_a, *fine),
            inward(weight_a),
        )
        sum_wa, sum_ba, sum_wb, sum_bb = summed_grads(
            part_wa, part_ba, part_wb, part_bb, (scale_a, scale_b)
        )
    grad_input = lax.all_to_all(
        grad_slab.reshape(c1, planes, rows, depth), "gz", split_axis=3, concat_axis=1, tiled=True
    )
    return (
        features.reshape(cotangent.shape),
        grad_input,
        sum_wa.reshape(weight_a.shape),
        sum_ba.reshape(c2),
        sum_wb.reshape(weight_b.shape),
        sum_bb.reshape(c3),
    )


def solution(mesh):
    return jax.shard_map(
        on_device,
        mesh=mesh,
        in_specs=(P(None, "gx", "gy", "gz"), P(), P(), P(), P(), P(None, ("gx", "gz"), "gy", None)),
        out_specs=(
            P(None, ("gx", "gz"), "gy", None),
            P(None, "gx", "gy", "gz"),
            P(),
            P(),
            P(),
            P(),
        ),
        check_vma=False,
    )
```

profile of v0, /device:TPU:1, one launch (start us, length us, event | category | flops | bytes accessed | tf_op | source)
XLA Modules:
  0.0 215.1 jit_solution(14522417750021422432)
XLA Ops:
  0.6 3.2 %copy.39 = bf16[32,32,8,16]{0,3,2,1:T(8,128)(2,1)S(1)} copy(bf16[32,32,8,16]{1,3,2,0:T(8,128)(2,1)} %param.6) | data formatting | bytes 524288 | tf_op args[0]
  4.9 21.4 %all_to_all.33 = bf16[16,2,4096]{2,1,0:T(2,128)(2,1)S(1)} all-to-all(bf16[16,2,4096]{2,1,0:T(2,128)(2,1)S(1)} %reshape.138), channel_id=1, replica_groups=mesh['gx'=2,'gy'=8,'gz'=16] {'gz'}, dimensions={0} | all-to-all | bytes 524288 | tf_op jit(solution)/shard_map/all_to_all | solution.py:558
  27.8 1.9 collective-permute-start
  29.7 2.4 %collective-permute-start.1 = (bf16[32,2048]{0,1:T(8,128)(2,1)S(1)}, bf16[32,2048]{0,1:T(8,128)(2,1)S(1)}, u32[]{:S(2)}, u32[]{:S(2)}) collective-permute-start(bf16[32,2048]{0,1:T(8,128)(2,1)S(1)} %get-tuple-element.51), channel_id=1, source_target_pairs={{1,0},{2,1},{3,2},{4,3},{5,4},{6,5},{7,6},{8,7},{9,8},{10,9},{11,1... | collective-permute-start | bytes 393224 | tf_op jit(solution)/shard_map/ppermute | solution.py:24
  32.5 3.6 %collective-permute-done = bf16[32,2048]{0,1:T(8,128)(2,1)S(1)} collective-permute-done((bf16[32,2048]{0,1:T(8,128)(2,1)}, bf16[32,2048]{0,1:T(8,128)(2,1)S(1)}, u32[]{:S(2)}, u32[]{:S(2)}) %collective-permute-start) | collective-permute-done | bytes 131104 | tf_op jit(solution)/shard_map/ppermute | solution.py:23
  36.4 3.9 %collective-permute-done.1 = bf16[32,2048]{0,1:T(8,128)(2,1)S(1)} collective-permute-done((bf16[32,2048]{0,1:T(8,128)(2,1)S(1)}, bf16[32,2048]{0,1:T(8,128)(2,1)S(1)}, u32[]{:S(2)}, u32[]{:S(2)}) %collective-permute-start.1) | collective-permute-done | bytes 131104 | tf_op jit(solution)/shard_map/ppermute | solution.py:24
  40.8 3.5 %collective-permute-start.2 = (bf16[32,4,1,256]{3,2,1,0:T(2,128)(2,1)S(1)}, bf16[32,4,1,256]{3,2,1,0:T(2,128)(2,1)S(1)}, u32[]{:S(2)}, u32[]{:S(2)}) collective-permute-start(bf16[32,4,1,256]{3,2,1,0:T(2,128)(2,1)S(1)} %get-tuple-element.54), channel_id=1, source_target_pairs={{0,16},{16,32},{32,48},{48,64},{64,80},{80,96},{96,112},{1,17},{17... | collective-permute-start | bytes 196616 | tf_op jit(solution)/shard_map/ppermute | solution.py:23
  46.2 3.8 %collective-permute-done.3 = bf16[32,4,1,256]{3,2,1,0:T(2,128)(2,1)S(1)} collective-permute-done((bf16[32,4,1,256]{3,2,1,0:T(2,128)(2,1)S(1)}, bf16[32,4,1,256]{3,2,1,0:T(2,128)(2,1)S(1)}, u32[]{:S(2)}, u32[]{:S(2)}) %collective-permute-start.3) | collective-permute-done | bytes 65568 | tf_op jit(solution)/shard_map/ppermute | solution.py:24
  52.9 4.0 %collective-permute-start.4 = (bf16[64,512]{1,0:T(8,128)(2,1)S(1)}, bf16[64,512]{1,0:T(8,128)(2,1)S(1)}, u32[]{:S(2)}, u32[]{:S(2)}) collective-permute-start(bf16[64,512]{1,0:T(8,128)(2,1)S(1)} %get-tuple-element.18), channel_id=1, source_target_pairs={{0,1},{1,2},{2,3},{3,4},{4,5},{5,6},{6,7},{7,8},{8,9},{9,10},{10,1... | collective-permute-start | bytes 196616 | tf_op jit(solution)/shard_map/ppermute | solution.py:23
  56.9 1.9 collective-permute-start.5
  58.8 3.6 %collective-permute-done.5 = bf16[64,512]{1,0:T(8,128)(2,1)S(1)} collective-permute-done((bf16[64,512]{1,0:T(8,128)(2,1)S(1)}, bf16[64,512]{1,0:T(8,128)(2,1)S(1)}, u32[]{:S(2)}, u32[]{:S(2)}) %collective-permute-start.5) | collective-permute-done | bytes 65568 | tf_op jit(solution)/shard_map/ppermute | solution.py:24
  62.7 3.2 %collective-permute-start.6 = (bf16[64,3,1,128]{3,2,1,0:T(2,128)(2,1)S(1)}, bf16[64,3,1,128]{3,2,1,0:T(2,128)(2,1)S(1)}, u32[]{:S(2)}, u32[]{:S(2)}) collective-permute-start(bf16[64,3,1,128]{3,2,1,0:T(2,128)(2,1)S(1)} %get-tuple-element.58), channel_id=1, source_target_pairs={{0,16},{16,32},{32,48},{48,64},{64,80},{80,96},{96,112},{1,17},{17... | collective-permute-start | bytes 147464 | tf_op jit(solution)/shard_map/ppermute | solution.py:23
  67.6 3.8 %collective-permute-done.7 = bf16[64,3,1,128]{3,2,1,0:T(2,128)(2,1)} collective-permute-done((bf16[64,3,1,128]{3,2,1,0:T(2,128)(2,1)S(1)}, bf16[64,3,1,128]{3,2,1,0:T(2,128)(2,1)}, u32[]{:S(2)}, u32[]{:S(2)}) %collective-permute-start.7) | collective-permute-done | bytes 49184 | tf_op jit(solution)/shard_map/ppermute | solution.py:24
  76.3 4.1 %collective-permute-start.8 = (bf16[128,512]{1,0:T(8,128)(2,1)S(1)}, bf16[128,512]{1,0:T(8,128)(2,1)S(1)}, u32[]{:S(2)}, u32[]{:S(2)}) collective-permute-start(bf16[128,512]{1,0:T(8,128)(2,1)S(1)} %get-tuple-element.20), channel_id=1, source_target_pairs={{0,1},{1,2},{2,3},{3,4},{4,5},{5,6},{6,7},{7,8},{8,9},{9,10},{10,1... | collective-permute-start | bytes 393224 | tf_op jit(solution)/shard_map/ppermute | solution.py:23
  80.4 1.9 collective-permute-start.9
  82.3 4.3 %collective-permute-done.9 = bf16[128,512]{1,0:T(8,128)(2,1)S(1)} collective-permute-done((bf16[128,512]{1,0:T(8,128)(2,1)S(1)}, bf16[128,512]{1,0:T(8,128)(2,1)S(1)}, u32[]{:S(2)}, u32[]{:S(2)}) %collective-permute-start.9) | collective-permute-done | bytes 131104 | tf_op jit(solution)/shard_map/ppermute | solution.py:24
  87.6 6.9 %collective-permute-start.10 = (bf16[128,3,1,128]{0,3,2,1:T(8,128)(2,1)}, bf16[128,3,1,128]{0,3,2,1:T(8,128)(2,1)S(1)}, u32[]{:S(2)}, u32[]{:S(2)}) collective-permute-start(bf16[128,3,1,128]{0,3,2,1:T(8,128)(2,1)} %get-tuple-element.56), channel_id=1, source_target_pairs={{0,16},{16,32},{32,48},{48,64},{64,80},{80,96},{96,112},{1,17},{17... | collective-permute-start | bytes 294920 | tf_op jit(solution)/shard_map/ppermute | solution.py:23
  96.6 4.2 %collective-permute-done.11 = bf16[128,3,1,128]{0,3,2,1:T(8,128)(2,1)} collective-permute-done((bf16[128,3,1,128]{0,3,2,1:T(8,128)(2,1)}, bf16[128,3,1,128]{0,3,2,1:T(8,128)(2,1)}, u32[]{:S(2)}, u32[]{:S(2)}) %collective-permute-start.11) | collective-permute-done | bytes 98336 | tf_op jit(solution)/shard_map/ppermute | solution.py:24
  100.8 1.8 pad_maximum_fusion.3
  105.0 3.9 %collective-permute-start.12 = (bf16[64,2048]{1,0:T(8,128)(2,1)S(1)}, bf16[64,2048]{1,0:T(8,128)(2,1)S(1)}, u32[]{:S(2)}, u32[]{:S(2)}) collective-permute-start(bf16[64,2048]{1,0:T(8,128)(2,1)S(1)} %get-tuple-element.52), channel_id=1, source_target_pairs={{0,1},{1,2},{2,3},{3,4},{4,5},{5,6},{6,7},{7,8},{8,9},{9,10},{10,1... | collective-permute-start | bytes 786440 | tf_op jit(solution)/shard_map/ppermute | solution.py:23
  108.9 1.9 collective-permute-start.13
  112.2 4.4 %collective-permute-done.13 = bf16[64,2048]{1,0:T(8,128)(2,1)S(1)} collective-permute-done((bf16[64,2048]{1,0:T(8,128)(2,1)S(1)}, bf16[64,2048]{1,0:T(8,128)(2,1)S(1)}, u32[]{:S(2)}, u32[]{:S(2)}) %collective-permute-start.13) | collective-permute-done | bytes 262176 | tf_op jit(solution)/shard_map/ppermute | solution.py:24
  118.1 4.4 %collective-permute-start.14 = (bf16[64,4,1,256]{3,2,1,0:T(2,128)(2,1)}, bf16[64,4,1,256]{3,2,1,0:T(2,128)(2,1)S(1)}, u32[]{:S(2)}, u32[]{:S(2)}) collective-permute-start(bf16[64,4,1,256]{3,2,1,0:T(2,128)(2,1)} %get-tuple-element.48), channel_id=1, source_target_pairs={{0,16},{16,32},{32,48},{48,64},{64,80},{80,96},{96,112},{1,17},{17... | collective-permute-start | bytes 393224 | tf_op jit(solution)/shard_map/ppermute | solution.py:23
  124.2 1.9 collective-permute-done.14
  126.1 4.3 %collective-permute-done.15 = bf16[64,4,1,256]{3,2,1,0:T(2,128)(2,1)S(1)} collective-permute-done((bf16[64,4,1,256]{3,2,1,0:T(2,128)(2,1)}, bf16[64,4,1,256]{3,2,1,0:T(2,128)(2,1)S(1)}, u32[]{:S(2)}, u32[]{:S(2)}) %collective-permute-start.15) | collective-permute-done | bytes 131104 | tf_op jit(solution)/shard_map/ppermute | solution.py:24
  130.4 2.9 %pad_maximum_fusion = bf16[64,4,10,256]{3,2,1,0:T(8,128)(2,1)} fusion(bf16[64,4,1,256]{3,2,1,0:T(2,128)(2,1)S(1)} %collective-permute-done.15, bf16[64,4,8,256]{3,2,1,0:T(8,128)(2,1)S(1)} %bitcast.57, bf16[64,4,1,256]{3,2,1,0:T(2,128)(2,1)S(1)} %collective-permute-done.14), kind=kLoop, calls=%fused_computation | loop fusion | flops 3932160 | bytes 2621440 | tf_op jit(solution)/shard_map/concatenate | solution.py:39
  133.3 2.7 %reshape.130.wide_ref = bf16[64,10240]{1,0:T(8,128)(2,1)S(1)} reshape(bf16[64,4,10,256]{3,2,1,0:T(8,128)(2,1)} %pad_maximum_fusion) | data formatting | bytes 2621440 | tf_op jit(solution)/shard_map/reshape | solution.py:39
  136.0 2.6 %shard_map.112 = bf16[32,4096]{1,0:T(8,128)(2,1)S(1)} custom-call(bf16[64,10240]{1,0:T(8,128)(2,1)S(1)} %reshape.130.wide_ref, bf16[32,1728]{1,0:T(8,128)(2,1)S(1)} %reshape.132.weight_ref), custom_call_target="tpu_custom_call" | custom-call | flops 452984832 | bytes 1421312 | tf_op jit(solution)/shard_map/pallas_call | solution.py:135
  141.4 10.0 %all-to-all-start.1 = ((bf16[16,2,4096]{2,1,0:T(2,128)(2,1)}), bf16[16,2,4096]{2,1,0:T(2,128)(2,1)S(1)}, u32[]{:S(2)}, u32[]{:S(2)}) async-start(bf16[16,2,4096]{2,1,0:T(2,128)(2,1)} %reshape.140), calls=%async_computation.1 | async-start | bytes 524288 | tf_op jit(solution)/shard_map/all_to_all | solution.py:624
  152.1 2.2 %shard_map.113 = (f32[864,64]{1,0:T(8,128)S(1)}, f32[8,64]{1,0:T(8,128)S(1)}) custom-call(bf16[32,10240]{1,0:T(8,128)(2,1)S(1)} %reshape.118.wide_ref, bf16[64,4096]{1,0:T(8,128)(2,1)S(1)} %shard_map.111.grad_ref), custom_call_target="tpu_custom_call" | custom-call | flops 452984832 | bytes 1179648 | tf_op jit(solution)/shard_map/pallas_call | solution.py:135
  155.6 53.0 %shard_map.114 = (f32[864,64]{1,0:T(8,128)}, f32[1,64]{1,0:T(1,128)}, f32[1728,128]{1,0:T(8,128)}, f32[1,128]{1,0:T(1,128)}) custom-call(f32[864,64]{1,0:T(8,128)} %copy-done.1, f32[8,64]{1,0:T(8,128)} %copy-done.5, f32[1728,128]{1,0:T(8,128)} %copy-done, f32[8,128]{1,0:T(8,128)} %copy-done.4), custom_call_target="tpu_custom_call" | custom-call | tf_op jit(solution)/shard_map/pallas_call | solution.py:243
  209.5 2.9 %copy.58 = bf16[32,32,8,16]{1,3,2,0:T(8,128)(2,1)} copy(bf16[32,32,8,16]{0,3,2,1:T(8,128)(2,1)S(1)} %bitcast.63) | data formatting | bytes 524288
  (95 shorter events, 33.2 us)
Async XLA Ops:
  27.8 8.3 %collective-permute-start = (bf16[32,2048]{0,1:T(8,128)(2,1)}, bf16[32,2048]{0,1:T(8,128)(2,1)S(1)}, u32[]{:S(2)}, u32[]{:S(2)}) collective-permute-start(bf16[32,2048]{0,1:T(8,128)(2,1)} %get-tuple-element.50), channel_id=1, source_target_pairs={{0,1},{1,2},{2,3},{3,4},{4,5},{5,6},{6,7},{7,8},{8,9},{9,10},{10,1... | collective-permute-start | bytes 393224 | tf_op jit(solution)/shard_map/ppermute | solution.py:23
  29.7 10.5 %collective-permute-start.1 = (bf16[32,2048]{0,1:T(8,128)(2,1)S(1)}, bf16[32,2048]{0,1:T(8,128)(2,1)S(1)}, u32[]{:S(2)}, u32[]{:S(2)}) collective-permute-start(bf16[32,2048]{0,1:T(8,128)(2,1)S(1)} %get-tuple-element.51), channel_id=1, source_target_pairs={{1,0},{2,1},{3,2},{4,3},{5,4},{6,5},{7,6},{8,7},{9,8},{10,9},{11,1... | collective-permute-start | bytes 393224 | tf_op jit(solution)/shard_map/ppermute | solution.py:24
  32.5 13.2 %copy-start.8 = (bf16[3,3,3,32,64]{4,3,2,1,0:T(8,128)(2,1)S(1)}, bf16[3,3,3,32,64]{4,3,2,1,0:T(8,128)(2,1)}, u32[]{:S(2)}) copy-start(bf16[3,3,3,32,64]{4,3,2,1,0:T(8,128)(2,1)} %param.7) | copy-start | bytes 331780
  32.5 13.3 %copy-start.12 = (f32[64]{0:T(128)S(1)}, f32[64]{0:T(128)}, u32[]{:S(2)}) copy-start(f32[64]{0:T(128)} %param.8) | copy-start | bytes 772
  40.8 5.4 %collective-permute-start.2 = (bf16[32,4,1,256]{3,2,1,0:T(2,128)(2,1)S(1)}, bf16[32,4,1,256]{3,2,1,0:T(2,128)(2,1)S(1)}, u32[]{:S(2)}, u32[]{:S(2)}) collective-permute-start(bf16[32,4,1,256]{3,2,1,0:T(2,128)(2,1)S(1)} %get-tuple-element.54), channel_id=1, source_target_pairs={{0,16},{16,32},{32,48},{48,64},{64,80},{80,96},{96,112},{1,17},{17... | collective-permute-start | bytes 196616 | tf_op jit(solution)/shard_map/ppermute | solution.py:23
  44.3 5.7 %collective-permute-start.3 = (bf16[32,4,1,256]{3,2,1,0:T(2,128)(2,1)S(1)}, bf16[32,4,1,256]{3,2,1,0:T(2,128)(2,1)S(1)}, u32[]{:S(2)}, u32[]{:S(2)}) collective-permute-start(bf16[32,4,1,256]{3,2,1,0:T(2,128)(2,1)S(1)} %get-tuple-element.55), channel_id=1, source_target_pairs={{16,0},{32,16},{48,32},{64,48},{80,64},{96,80},{112,96},{17,1},{33... | collective-permute-start | bytes 196616 | tf_op jit(solution)/shard_map/ppermute | solution.py:24
  50.7 16.5 %copy-start.6 = (bf16[3,3,3,64,128]{4,3,2,1,0:T(8,128)(2,1)S(1)}, bf16[3,3,3,64,128]{4,3,2,1,0:T(8,128)(2,1)}, u32[]{:S(2)}) copy-start(bf16[3,3,3,64,128]{4,3,2,1,0:T(8,128)(2,1)} %param.9) | copy-start | bytes 1327108
  51.1 16.3 %copy-start.11 = (bf16[128,1,4,128]{3,2,1,0:T(4,128)(2,1)S(1)}, bf16[128,1,4,128]{3,2,1,0:T(4,128)(2,1)}, u32[]{:S(2)}) copy-start(bf16[128,1,4,128]{3,2,1,0:T(4,128)(2,1)} %param.11) | copy-start | bytes 393220
  51.1 16.4 %copy-start.13 = (f32[128]{0:T(128)S(1)}, f32[128]{0:T(128)}, u32[]{:S(2)}) copy-start(f32[128]{0:T(128)} %param.10) | copy-start | bytes 1540
  52.9 6.0 %collective-permute-start.4 = (bf16[64,512]{1,0:T(8,128)(2,1)S(1)}, bf16[64,512]{1,0:T(8,128)(2,1)S(1)}, u32[]{:S(2)}, u32[]{:S(2)}) collective-permute-start(bf16[64,512]{1,0:T(8,128)(2,1)S(1)} %get-tuple-element.18), channel_id=1, source_target_pairs={{0,1},{1,2},{2,3},{3,4},{4,5},{5,6},{6,7},{7,8},{8,9},{9,10},{10,1... | collective-permute-start | bytes 196616 | tf_op jit(solution)/shard_map/ppermute | solution.py:23
  56.9 5.6 %collective-permute-start.5 = (bf16[64,512]{1,0:T(8,128)(2,1)S(1)}, bf16[64,512]{1,0:T(8,128)(2,1)S(1)}, u32[]{:S(2)}, u32[]{:S(2)}) collective-permute-start(bf16[64,512]{1,0:T(8,128)(2,1)S(1)} %get-tuple-element.18), channel_id=1, source_target_pairs={{1,0},{2,1},{3,2},{4,3},{5,4},{6,5},{7,6},{8,7},{9,8},{10,9},{11,1... | collective-permute-start | bytes 196616 | tf_op jit(solution)/shard_map/ppermute | solution.py:24
  62.7 4.9 %collective-permute-start.6 = (bf16[64,3,1,128]{3,2,1,0:T(2,128)(2,1)S(1)}, bf16[64,3,1,128]{3,2,1,0:T(2,128)(2,1)S(1)}, u32[]{:S(2)}, u32[]{:S(2)}) collective-permute-start(bf16[64,3,1,128]{3,2,1,0:T(2,128)(2,1)S(1)} %get-tuple-element.58), channel_id=1, source_target_pairs={{0,16},{16,32},{32,48},{48,64},{64,80},{80,96},{96,112},{1,17},{17... | collective-permute-start | bytes 147464 | tf_op jit(solution)/shard_map/ppermute | solution.py:23
  65.9 5.5 %collective-permute-start.7 = (bf16[64,3,1,128]{3,2,1,0:T(2,128)(2,1)S(1)}, bf16[64,3,1,128]{3,2,1,0:T(2,128)(2,1)}, u32[]{:S(2)}, u32[]{:S(2)}) collective-permute-start(bf16[64,3,1,128]{3,2,1,0:T(2,128)(2,1)S(1)} %get-tuple-element.59), channel_id=1, source_target_pairs={{16,0},{32,16},{48,32},{64,48},{80,64},{96,80},{112,96},{17,1},{33... | collective-permute-start | bytes 147464 | tf_op jit(solution)/shard_map/ppermute | solution.py:24
  74.1 0.9 copy-start
  75.0 0.7 copy-start.2
  75.7 0.6 copy-start.4
  76.3 6.0 %collective-permute-start.8 = (bf16[128,512]{1,0:T(8,128)(2,1)S(1)}, bf16[128,512]{1,0:T(8,128)(2,1)S(1)}, u32[]{:S(2)}, u32[]{:S(2)}) collective-permute-start(bf16[128,512]{1,0:T(8,128)(2,1)S(1)} %get-tuple-element.20), channel_id=1, source_target_pairs={{0,1},{1,2},{2,3},{3,4},{4,5},{5,6},{6,7},{7,8},{8,9},{9,10},{10,1... | collective-permute-start | bytes 393224 | tf_op jit(solution)/shard_map/ppermute | solution.py:23
  80.4 6.3 %collective-permute-start.9 = (bf16[128,512]{1,0:T(8,128)(2,1)S(1)}, bf16[128,512]{1,0:T(8,128)(2,1)S(1)}, u32[]{:S(2)}, u32[]{:S(2)}) collective-permute-start(bf16[128,512]{1,0:T(8,128)(2,1)S(1)} %get-tuple-element.20), channel_id=1, source_target_pairs={{1,0},{2,1},{3,2},{4,3},{5,4},{6,5},{7,6},{8,7},{9,8},{10,9},{11,1... | collective-permute-start | bytes 393224 | tf_op jit(solution)/shard_map/ppermute | solution.py:24
  87.6 9.0 %collective-permute-start.10 = (bf16[128,3,1,128]{0,3,2,1:T(8,128)(2,1)}, bf16[128,3,1,128]{0,3,2,1:T(8,128)(2,1)S(1)}, u32[]{:S(2)}, u32[]{:S(2)}) collective-permute-start(bf16[128,3,1,128]{0,3,2,1:T(8,128)(2,1)} %get-tuple-element.56), channel_id=1, source_target_pairs={{0,16},{16,32},{32,48},{48,64},{64,80},{80,96},{96,112},{1,17},{17... | collective-permute-start | bytes 294920 | tf_op jit(solution)/shard_map/ppermute | solution.py:23
  94.5 6.2 %collective-permute-start.11 = (bf16[128,3,1,128]{0,3,2,1:T(8,128)(2,1)}, bf16[128,3,1,128]{0,3,2,1:T(8,128)(2,1)}, u32[]{:S(2)}, u32[]{:S(2)}) collective-permute-start(bf16[128,3,1,128]{0,3,2,1:T(8,128)(2,1)} %get-tuple-element.57), channel_id=1, source_target_pairs={{16,0},{32,16},{48,32},{64,48},{80,64},{96,80},{112,96},{17,1},{33... | collective-permute-start | bytes 294920 | tf_op jit(solution)/shard_map/ppermute | solution.py:24
  105.0 7.2 %collective-permute-start.12 = (bf16[64,2048]{1,0:T(8,128)(2,1)S(1)}, bf16[64,2048]{1,0:T(8,128)(2,1)S(1)}, u32[]{:S(2)}, u32[]{:S(2)}) collective-permute-start(bf16[64,2048]{1,0:T(8,128)(2,1)S(1)} %get-tuple-element.52), channel_id=1, source_target_pairs={{0,1},{1,2},{2,3},{3,4},{4,5},{5,6},{6,7},{7,8},{8,9},{9,10},{10,1... | collective-permute-start | bytes 786440 | tf_op jit(solution)/shard_map/ppermute | solution.py:23
  108.9 7.7 %collective-permute-start.13 = (bf16[64,2048]{1,0:T(8,128)(2,1)S(1)}, bf16[64,2048]{1,0:T(8,128)(2,1)S(1)}, u32[]{:S(2)}, u32[]{:S(2)}) collective-permute-start(bf16[64,2048]{1,0:T(8,128)(2,1)S(1)} %get-tuple-element.53), channel_id=1, source_target_pairs={{1,0},{2,1},{3,2},{4,3},{5,4},{6,5},{7,6},{8,7},{9,8},{10,9},{11,1... | collective-permute-start | bytes 786440 | tf_op jit(solution)/shard_map/ppermute | solution.py:24
  116.7 7.1 %copy-start.9 = (bf16[3,3,3,32,64]{4,3,2,1,0:T(8,128)(2,1)S(1)}, bf16[3,3,3,32,64]{4,3,2,1,0:T(8,128)(2,1)}, u32[]{:S(2)}) copy-start(bf16[3,3,3,32,64]{4,3,2,1,0:T(8,128)(2,1)} %param.7) | copy-start | bytes 331780
  118.1 8.0 %collective-permute-start.14 = (bf16[64,4,1,256]{3,2,1,0:T(2,128)(2,1)}, bf16[64,4,1,256]{3,2,1,0:T(2,128)(2,1)S(1)}, u32[]{:S(2)}, u32[]{:S(2)}) collective-permute-start(bf16[64,4,1,256]{3,2,1,0:T(2,128)(2,1)} %get-tuple-element.48), channel_id=1, source_target_pairs={{0,16},{16,32},{32,48},{48,64},{64,80},{80,96},{96,112},{1,17},{17... | collective-permute-start | bytes 393224 | tf_op jit(solution)/shard_map/ppermute | solution.py:23
  122.5 7.9 %collective-permute-start.15 = (bf16[64,4,1,256]{3,2,1,0:T(2,128)(2,1)}, bf16[64,4,1,256]{3,2,1,0:T(2,128)(2,1)S(1)}, u32[]{:S(2)}, u32[]{:S(2)}) collective-permute-start(bf16[64,4,1,256]{3,2,1,0:T(2,128)(2,1)} %get-tuple-element.49), channel_id=1, source_target_pairs={{16,0},{32,16},{48,32},{64,48},{80,64},{96,80},{112,96},{17,1},{33... | collective-permute-start | bytes 393224 | tf_op jit(solution)/shard_map/ppermute | solution.py:24
  138.6 12.8 %copy-start.3 = (bf16[128,512]{1,0:T(8,128)(2,1)S(1)}, bf16[128,512]{1,0:T(8,128)(2,1)}, u32[]{:S(2)}) copy-start(bf16[128,512]{1,0:T(8,128)(2,1)} %copy-done.2) | copy-start | bytes 393220
  141.4 67.2 %all-to-all-start.1 = ((bf16[16,2,4096]{2,1,0:T(2,128)(2,1)}), bf16[16,2,4096]{2,1,0:T(2,128)(2,1)S(1)}, u32[]{:S(2)}, u32[]{:S(2)}) async-start(bf16[16,2,4096]{2,1,0:T(2,128)(2,1)} %reshape.140), calls=%async_computation.1 | async-start | bytes 524288 | tf_op jit(solution)/shard_map/all_to_all | solution.py:624
  154.3 0.8 copy-start.1
  209.2 3.2 %copy-start.10 = (f32[864,64]{1,0:T(8,128)S(1)}, f32[864,64]{1,0:T(8,128)}, u32[]{:S(2)}) copy-start(f32[864,64]{1,0:T(8,128)} %get-tuple-element.26) | copy-start | bytes 663556
  209.2 4.0 %copy-start.15 = (f32[1,64]{1,0:T(1,128)S(1)}, f32[1,64]{1,0:T(1,128)}, u32[]{:S(2)}) copy-start(f32[1,64]{1,0:T(1,128)} %get-tuple-element.27) | copy-start | bytes 772
  209.5 4.2 %copy-start.7 = (f32[1728,128]{1,0:T(8,128)S(1)}, f32[1728,128]{1,0:T(8,128)}, u32[]{:S(2)}) copy-start(f32[1728,128]{1,0:T(8,128)} %get-tuple-element.28) | copy-start | bytes 2654212
  209.5 5.1 %copy-start.14 = (f32[1,128]{1,0:T(1,128)S(1)}, f32[1,128]{1,0:T(1,128)}, u32[]{:S(2)}) copy-start(f32[1,128]{1,0:T(1,128)} %get-tuple-element.29) | copy-start | bytes 1540
  (1 other events, 0.6 us)
where the time goes:
time: 216 us; the launch traced here: 215 us
  Pallas kernels  61.8 us (29%)
  starting transfers between devices  55.5 us (26%)
  waiting for transfers between devices  39.5 us (18%)
  local copies, waits for them, and re-layouts  29 us (13%)
  blocking collectives  21.4 us (10%)
  other arithmetic  6.83 us (3%)
    pallas_call x1, Pallas kernels, summed_grads(): pl.pallas_call(functools.partial(sum_kernel, steps, halvings, rows, scale...  53 us
    ppermute x8, waiting for transfers between devices, shared(): lax.ppermute(lax.slice_in_dim(block, 0, width, axis=dim), axis, backward)  32.3 us
    ppermute x8, starting transfers between devices, shared(): lax.ppermute(lax.slice_in_dim(block, last - width, last, axis=dim), axis,...  32 us
    all_to_all x1, blocking collectives, on_device(): lax.all_to_all(volume, 'gz', split_axis=1, concat_axis=3, tiled=True)  21.4 us
    unnamed x47, local copies, waits for them, and re-layouts  16.7 us
    ppermute x8, starting transfers between devices, shared(): lax.ppermute(lax.slice_in_dim(block, 0, width, axis=dim), axis, backward)  13.5 us
    all_to_all x1, starting transfers between devices, on_device(): lax.all_to_all(grad_slab.reshape(c1, planes, rows, depth), 'gz', split_ax...  9.98 us
    pallas_call x5, Pallas kernels, local_kernel(): pl.pallas_call(body, out_shape=[jax.ShapeDtypeStruct(shape, dtype) for sh...  8.76 us
  transfers between devices with their start and end apart: 17, of which 12 were waited for; matrix products, arithmetic and copies ran while one was open for 1% of the time, Pallas kernels for 26%

commit v1 on v0

v1 whole, which is shorter than its diff:
```python
import functools
import math

import jax
import jax.numpy as jnp
from jax import lax
from jax.experimental import pallas as pl
from jax.experimental.pallas import tpu as pltpu
from jax.sharding import PartitionSpec as P

MESH = pl.DeviceIdType.MESH


def slope_of(value):
    sigma = jax.nn.sigmoid(value)
    return sigma + value * sigma * (1.0 - sigma)


def put_windows(wide_ref, windows, planes, rows, depth):
    wide = wide_ref[...]
    width, extent = wide.shape
    place = lax.broadcasted_iota(jnp.int32, (width, extent), 1) % depth
    loose = wide.astype(jnp.float32)
    before = jnp.where(place == 0, 0.0, pltpu.roll(loose, 1, 1)).astype(jnp.bfloat16)
    after = jnp.where(place == depth - 1, 0.0, pltpu.roll(loose, extent - 1, 1)).astype(jnp.bfloat16)
    size = rows * depth
    for third, moved in enumerate((before, wide, after)):
        for first in range(3):
            for second in range(3):
                at = (first * 9 + second * 3 + third) * width
                for plane in range(planes):
                    begin = ((plane + first) * (rows + 2) + second) * depth
                    windows[at : at + width, plane * size : (plane + 1) * size] = moved[
                        :, begin : begin + size
                    ]


def dot_rows(left, right):
    return lax.dot_general(
        left, right, (((1,), (1,)), ((), ())), preferred_element_type=jnp.float32
    )


def forward_a_kernel(dims, wide_ref, weight_ref, bias_ref, pool_ref, before_ref, pooled_ref, windows):
    planes, rows, depth = dims
    put_windows(wide_ref, windows, *dims)
    before = jnp.dot(weight_ref[...], windows[...], preferred_element_type=jnp.float32)
    before = before + bias_ref[...]
    before_ref[...] = before
    active = before * jax.nn.sigmoid(before)
    size = rows * depth
    for row in range(rows // 2):
        parts = [
            active[:, plane * size + (2 * row + j) * depth : plane * size + (2 * row + j + 1) * depth]
            for plane in range(planes)
            for j in range(2)
        ]
        summed = sum(parts[1:], parts[0])
        paired = jnp.dot(
            summed, pool_ref[...], precision=lax.Precision.HIGHEST, preferred_element_type=jnp.float32
        )
        pooled_ref[:, row * depth // 2 : (row + 1) * depth // 2] = (paired * 0.125).astype(jnp.bfloat16)


def middle_kernel(dims, wide_ref, weight_ref, bias_ref, cot_ref, feat_ref, grad_ref, wb_ref, bb_ref, windows):
    put_windows(wide_ref, windows, *dims)
    before = jnp.dot(weight_ref[...], windows[...], preferred_element_type=jnp.float32)
    before = before + bias_ref[...]
    feat_ref[...] = (before * jax.nn.sigmoid(before)).astype(jnp.bfloat16)
    grad = (cot_ref[...].astype(jnp.float32) * slope_of(before)).astype(jnp.bfloat16)
    grad_ref[...] = grad
    wb_ref[...] = dot_rows(windows[...], grad)
    bb_ref[...] = dot_rows(jnp.ones((8, grad.shape[1]), jnp.bfloat16), grad)


def backward_b_kernel(dims, fine, wide_ref, weight_ref, before_ref, spread_ref, grad_ref, windows):
    put_windows(wide_ref, windows, *dims)
    pooled = jnp.dot(weight_ref[...], windows[...], preferred_element_type=jnp.float32)
    pooled = pooled.astype(jnp.bfloat16)
    planes, rows, depth = fine
    size = rows * depth
    for row in range(rows // 2):
        part = pooled[:, row * depth // 2 : (row + 1) * depth // 2]
        spread = jnp.dot(part, spread_ref[...], preferred_element_type=jnp.float32) * 0.125
        for plane in range(planes):
            for j in range(2):
                begin = plane * size + (2 * row + j) * depth
                slope = slope_of(before_ref[:, begin : begin + depth])
                grad_ref[:, begin : begin + depth] = (spread * slope).astype(jnp.bfloat16)


def backward_a_kernel(dims, wide_ref, weight_ref, out_ref, windows):
    put_windows(wide_ref, windows, *dims)
    out = jnp.dot(weight_ref[...], windows[...], preferred_element_type=jnp.float32)
    out_ref[...] = out.astype(jnp.bfloat16)


class Halo:
    def __init__(self, wide, dims, where, sems, at):
        planes, rows, depth = dims
        stride = (rows + 2) * depth
        send, recv = sems
        line, lines, row, cuts, count = where
        self.moves = []
        for up in (-1, 0, 1):
            for side in (-1, 0, 1):
                if up == 0 and side == 0:
                    continue
                to_line, to_row = (line + up + lines) % lines, (row + side + cuts) % cuts
                goes = within(line + up, lines) & within(row + side, cuts)
                comes = within(line - up, lines) & within(row - side, cuts)
                source, target, extent = {
                    -1: (1, rows + 1, 1),
                    0: (1, 1, rows),
                    1: (rows, 0, 1),
                }[side]
                pairs = {
                    -1: [(1, planes + 1)],
                    0: [(p, p) for p in range(1, planes + 1)],
                    1: [(planes, 0)],
                }[up]
                for have, give in pairs:
                    begin, end = have * stride + source * depth, give * stride + target * depth
                    copy = pltpu.make_async_remote_copy(
                        src_ref=wide.at[:, begin : begin + extent * depth],
                        dst_ref=wide.at[:, end : end + extent * depth],
                        send_sem=send.at[at + len(self.moves)],
                        recv_sem=recv.at[at + len(self.moves)],
                        device_id={"gx": to_line // count, "gz": to_line % count, "gy": to_row},
                        device_id_type=MESH,
                    )
                    self.moves.append((copy, goes, comes))

    def start(self):
        for copy, goes, _ in self.moves:
            pl.when(goes)(copy.start)

    def wait(self):
        for copy, goes, comes in self.moves:
            pl.when(goes)(copy.wait_send)
            pl.when(comes)(copy.wait_recv)


def within(at, count):
    return (at >= 0) & (at < count)


class Summing:
    def __init__(self, acc, stage, first, mine, second, whole, sems):
        self.acc, self.stage, self.first = acc, stage, first
        self.mine, self.second, self.whole = mine, second, whole
        self.sems = sems
        gy = lax.axis_size("gy")
        self.count = lax.axis_size("gx") * gy
        self.depth = lax.axis_size("gz")
        self.me = lax.axis_index("gx") * gy + lax.axis_index("gy")
        self.level = lax.axis_index("gz")

    def across(self, phase, k, source, target):
        gy = lax.axis_size("gy")
        to = (self.me + k) % self.count
        return pltpu.make_async_remote_copy(
            src_ref=source(to),
            dst_ref=target,
            send_sem=self.sems.at[phase, 0, k],
            recv_sem=self.sems.at[phase, 1, k],
            device_id={"gx": to // gy, "gy": to % gy},
            device_id_type=MESH,
        )

    def along(self, k):
        return pltpu.make_async_remote_copy(
            src_ref=self.mine,
            dst_ref=self.second.at[self.level],
            send_sem=self.sems.at[1, 0, k],
            recv_sem=self.sems.at[1, 1, k],
            device_id={"gz": (self.level + k) % self.depth},
            device_id_type=MESH,
        )

    def scatters(self):
        return [
            self.across(0, k, lambda to: self.stage.at[to], self.first.at[self.me])
            for k in range(1, self.count)
        ]

    def alongs(self):
        return [self.along(k) for k in range(1, self.depth)]

    def gathers(self):
        here = self.whole.at[self.me]
        return [self.across(2, k, lambda to: here, here) for k in range(1, self.count)]

    def start(self):
        chunk = self.stage.shape[1]
        for i in range(self.count):
            self.stage[i] = self.acc[i * chunk : (i + 1) * chunk].astype(jnp.bfloat16)
        for copy in self.scatters():
            copy.start()
        self.first[self.me] = self.stage[self.me]

    def total(self, parts):
        total = parts[0].astype(jnp.float32)
        for i in range(1, parts.shape[0]):
            total = total + parts[i].astype(jnp.float32)
        return total.astype(jnp.bfloat16)

    def middle(self):
        for copy in self.scatters():
            copy.wait()
        part = self.total(self.first)
        self.mine[...] = part
        for copy in self.alongs():
            copy.start()
        self.second[self.level] = part

    def last(self):
        for copy in self.alongs():
            copy.wait()
        self.whole[self.me] = self.total(self.second)
        for copy in self.gathers():
            copy.start()

    def finish(self):
        for copy in self.gathers():
            copy.wait()


def place(wide, flat, dims):
    planes, rows, depth = dims
    size, stride = rows * depth, (rows + 2) * depth
    for plane in range(planes):
        begin = (plane + 1) * stride + depth
        wide[:, begin : begin + size] = flat[:, plane * size : (plane + 1) * size]


def greet():
    gx, gy, gz = [lax.axis_size(axis) for axis in ("gx", "gy", "gz")]
    me = lax.axis_index("gx") * gy + lax.axis_index("gy")
    level, row = lax.axis_index("gz"), lax.axis_index("gy")
    line = lax.axis_index("gx") * gz + level
    barrier = pltpu.get_barrier_semaphore()
    signal = lambda device: pl.semaphore_signal(barrier, inc=1, device_id=device, device_id_type=MESH)
    for k in range(1, gx * gy):
        to = (me + k) % (gx * gy)
        signal({"gx": to // gy, "gy": to % gy})
    for k in range(1, gz):
        signal({"gz": (level + k) % gz})
    for up in (-1, 0, 1):
        for side in (-1, 0, 1):
            if up or side:
                to, to_row = (line + up + gx * gz) % (gx * gz), (row + side + gy) % gy
                signal({"gx": to // gz, "gz": to % gz, "gy": to_row})
    pl.semaphore_wait(barrier, gx * gy + gz + 6)
    return line, gx * gz, row, gy, gz


def whole_kernel(setting, *refs):
    fine, coarse, scales = setting
    slab, w_a, b_a, pool, w_b, b_b, cot, v_b, spread, v_a = refs[:10]
    features, grad_slab, out_wa, out_ba, out_wb, out_bb = refs[10:16]
    wide_a, wide_b, wide_gb, wide_ga, win_a, win_b, win_gb, win_ga = refs[16:24]
    before_a, pooled, grad_b, grad_a, acc_a, acc_b = refs[24:30]
    parts_a, parts_b, sems = refs[30:35], refs[35:40], refs[40:]
    for wide in (wide_a, wide_b, wide_gb, wide_ga):
        wide[...] = jnp.zeros_like(wide)
    place(wide_a, slab, fine)
    where = greet()
    halos = [
        Halo(wide, dims, where, sems[:2], 10 * i)
        for i, (wide, dims) in enumerate(
            ((wide_a, fine), (wide_b, coarse), (wide_gb, coarse), (wide_ga, fine))
        )
    ]
    sum_a = Summing(acc_a, *parts_a, sems[2])
    sum_b = Summing(acc_b, *parts_b, sems[3])

    halos[0].start()
    halos[0].wait()
    forward_a_kernel(fine, wide_a, w_a, b_a, pool, before_a, pooled, win_a)
    place(wide_b, pooled, coarse)
    halos[1].start()
    halos[1].wait()
    top_b = out_wb.shape[0]
    middle_kernel(
        coarse, wide_b, w_b, b_b, cot, features, grad_b, acc_b.at[:top_b], acc_b.at[top_b : top_b + 8], win_b
    )
    place(wide_gb, grad_b, coarse)
    halos[2].start()
    acc_b[top_b + 8 :] = jnp.zeros((acc_b.shape[0] - top_b - 8, acc_b.shape[1]), jnp.float32)
    sum_b.start()
    halos[2].wait()
    backward_b_kernel(coarse, fine, wide_gb, v_b, before_a, spread, grad_a, win_gb)
    place(wide_ga, grad_a, fine)
    halos[3].start()
    grad = grad_a[...]
    half, width = out_wa.shape[0] // 2, out_wa.shape[1]
    acc_a[:half, :width] = dot_rows(win_a[:half], grad)
    acc_a[:half, width:] = dot_rows(win_a[half:], grad)
    acc_a[half:] = jnp.zeros((acc_a.shape[0] - half, acc_a.shape[1]), jnp.float32)
    acc_a[half : half + 8, :width] = dot_rows(jnp.ones((8, grad.shape[1]), jnp.bfloat16), grad)
    sum_a.start()
    sum_b.middle()
    halos[3].wait()
    backward_a_kernel(fine, wide_ga, v_a, grad_slab, win_ga)
    sum_a.middle()
    sum_b.last()
    sum_a.last()
    sum_b.finish()
    all_a, all_b = parts_a[4], parts_b[4]
    scale_a, scale_b = scales
    flat_b = all_b[...].astype(jnp.float32).reshape(-1, all_b.shape[2]) * scale_b
    out_wb[...] = flat_b[:top_b]
    out_bb[...] = flat_b[top_b : top_b + 1]
    sum_a.finish()
    flat_a = all_a[...].astype(jnp.float32).reshape(-1, all_a.shape[2]) * scale_a
    out_wa[:half] = flat_a[:half, :width]
    out_wa[half:] = flat_a[:half, width:]
    out_ba[...] = flat_a[half : half + 1, :width]


def between_exchanges(fine, coarse, scales, slab, weight_a, bias_a, weight_b, bias_b, cot, pool):
    f32, bf16 = jnp.float32, jnp.bfloat16
    c1, cells = slab.shape
    c2, c3 = weight_b.shape[3:]
    fewer = cells // 8
    members, levels = lax.axis_size("gx") * lax.axis_size("gy"), lax.axis_size("gz")
    rows_a = 27 * c1 // 2 + 16
    rows_a += -rows_a % (16 * members)
    rows_b = 27 * c2 + 16
    rows_b += -rows_b % (16 * members)
    extent = lambda dims: (dims[0] + 2) * (dims[1] + 2) * dims[2]
    setting = (fine, coarse, scales)
    buffers = []
    for rows in (rows_a, rows_b):
        chunk = rows // members
        buffers += [
            pltpu.VMEM((members, chunk, 128), bf16),
            pltpu.VMEM((members, chunk, 128), bf16),
            pltpu.VMEM((chunk, 128), bf16),
            pltpu.VMEM((levels, chunk, 128), bf16),
            pltpu.VMEM((members, chunk, 128), bf16),
        ]
    outs = [
        ((c3, fewer), bf16),
        ((c1, cells), bf16),
        ((27 * c1, c2), f32),
        ((1, c2), f32),
        ((27 * c2, c3), f32),
        ((1, c3), f32),
    ]
    operands = (
        slab,
        outward(weight_a),
        bias_a[:, None],
        pool,
        outward(weight_b),
        bias_b[:, None],
        cot,
        inward(weight_b),
        pool.T.astype(bf16),
        inward(weight_a),
    )
    most = max(members, levels)
    return pl.pallas_call(
        functools.partial(whole_kernel, setting),
        out_shape=[jax.ShapeDtypeStruct(shape, dtype) for shape, dtype in outs],
        in_specs=[pl.BlockSpec(memory_space=pltpu.VMEM)] * len(operands),
        out_specs=[pl.BlockSpec(memory_space=pltpu.VMEM)] * len(outs),
        scratch_shapes=[
            pltpu.VMEM((c1, extent(fine)), bf16),
            pltpu.VMEM((c2, extent(coarse)), bf16),
            pltpu.VMEM((c3, extent(coarse)), bf16),
            pltpu.VMEM((c2, extent(fine)), bf16),
            pltpu.VMEM((27 * c1, cells), bf16),
            pltpu.VMEM((27 * c2, fewer), bf16),
            pltpu.VMEM((27 * c3, fewer), bf16),
            pltpu.VMEM((27 * c2, cells), bf16),
            pltpu.VMEM((c2, cells), f32),
            pltpu.VMEM((c2, fewer), bf16),
            pltpu.VMEM((c3, fewer), bf16),
            pltpu.VMEM((c2, cells), bf16),
            pltpu.VMEM((rows_a, 128), f32),
            pltpu.VMEM((rows_b, 128), f32),
            *buffers,
            pltpu.SemaphoreType.DMA((40,)),
            pltpu.SemaphoreType.DMA((40,)),
            pltpu.SemaphoreType.DMA((3, 2, most)),
            pltpu.SemaphoreType.DMA((3, 2, most)),
        ],
        compiler_params=pltpu.CompilerParams(
            collective_id=1, has_side_effects=True, vmem_limit_bytes=60 * 2**20
        ),
    )(*operands)


def outward(weight):
    return weight.reshape(-1, weight.shape[-1]).T


def inward(weight):
    taps = weight[::-1, ::-1, ::-1].reshape(27, *weight.shape[3:])
    return jnp.transpose(taps, (1, 0, 2)).reshape(weight.shape[3], -1)


def on_device(volume, weight_a, bias_a, weight_b, bias_b, cotangent):
    f32, bf16 = jnp.float32, jnp.bfloat16
    count = lax.axis_size("gz")
    devices_all = lax.axis_size("gx") * lax.axis_size("gy") * count
    c1, nx, rows, nz = volume.shape
    cells = nx * rows * nz
    scale_a = 1.0 / math.sqrt(cells * devices_all)
    scale_b = 1.0 / math.sqrt(cells * devices_all // 8)
    c2, c3 = weight_b.shape[3:]
    planes, depth = nx // count, nz * count
    fine = (planes, rows, depth)
    coarse = (planes // 2, rows // 2, depth // 2)
    fewer = cells // 8
    pool = (jnp.arange(depth)[:, None] // 2 == jnp.arange(depth // 2)[None]).astype(f32)

    slab = lax.all_to_all(volume, "gz", split_axis=1, concat_axis=3, tiled=True).reshape(c1, cells)
    features, grad_slab, sum_wa, sum_ba, sum_wb, sum_bb = between_exchanges(
        fine,
        coarse,
        (scale_a, scale_b),
        slab,
        weight_a,
        bias_a,
        weight_b,
        bias_b,
        cotangent.reshape(c3, fewer),
        pool,
    )
    grad_input = lax.all_to_all(
        grad_slab.reshape(c1, planes, rows, depth), "gz", split_axis=3, concat_axis=1, tiled=True
    )
    return (
        features.reshape(cotangent.shape),
        grad_input,
        sum_wa.reshape(weight_a.shape),
        sum_ba.reshape(c2),
        sum_wb.reshape(weight_b.shape),
        sum_bb.reshape(c3),
    )


def solution(mesh):
    return jax.shard_map(
        on_device,
        mesh=mesh,
        in_specs=(P(None, "gx", "gy", "gz"), P(), P(), P(), P(), P(None, ("gx", "gz"), "gy", None)),
        out_specs=(
            P(None, ("gx", "gz"), "gy", None),
            P(None, "gx", "gy", "gz"),
            P(),
            P(),
            P(),
            P(),
        ),
        check_vma=False,
    )
```

time: 216 us -> 118 us (0.55)
  starting transfers between devices: 55.5 us -> 16.4 us
  waiting for transfers between devices: 39.5 us -> 13.6 us
  blocking collectives: 21.4 us -> 0 us
  other arithmetic: 6.83 us -> 1.4 us
  local copies, waits for them, and re-layouts: 29 us -> 25 us
    ppermute x16 -> x0, starting transfers between devices: 45.5 us -> none  [the longest x8 32 us: shared(): lax.ppermute(lax.slice_in_dim(block, last - width, last, axis=dim), axis,...]
    ppermute x16 -> x0, waiting for transfers between devices: 39.5 us -> none  [the longest x8 32.3 us: shared(): lax.ppermute(lax.slice_in_dim(block, 0, width, axis=dim), axis, backward)]
    all_to_all x1 -> x0, blocking collectives: 21.4 us -> none  [on_device(): lax.all_to_all(volume, 'gz', split_axis=1, concat_axis=3, tiled=True)]
    all_to_all x1, waiting for transfers between devices: 0.01 us -> 10.9 us  [on_device(): lax.all_to_all(grad_slab.reshape(c1, planes, rows, depth), 'gz', split_ax...]
    all_to_all x0 -> x1, starting transfers between devices: none -> 10.1 us  [on_device(): lax.all_to_all(volume, 'gz', split_axis=1, concat_axis=3, tiled=True)]
    concatenate x8 -> x0, other arithmetic: 6.72 us -> none  [the longest x4 6.57 us: widened(): jnp.concatenate([low, whole, high], axis=2).reshape(flat.shape[0], -1)]
    reshape x6 -> x0, local copies, waits for them, and re-layouts: 5.03 us -> none  [the longest x4 4.76 us: widened(): jnp.concatenate([low, whole, high], axis=2).reshape(flat.shape[0], -1)]
    all_to_all x1, starting transfers between devices: 9.98 us -> 6.33 us  [on_device(): lax.all_to_all(grad_slab.reshape(c1, planes, rows, depth), 'gz', split_ax...]
  transfers between devices with their start and end apart: 17 -> 2, of which waited for: 12 -> 2; matrix products, arithmetic and copies ran while one was open for 1% -> 7% of each run, Pallas kernels for 26% -> 0%
where the time goes in v1:
time: 118 us; the launch traced here: 117 us
  Pallas kernels  60.1 us (51%)
  local copies, waits for them, and re-layouts  25 us (21%)
  starting transfers between devices  16.4 us (14%)
  waiting for transfers between devices  13.6 us (12%)
  other arithmetic  1.4 us (1%)
    pallas_call x1, Pallas kernels, between_exchanges(): pl.pallas_call(functools.partial(whole_kernel, setting), out_shape=[jax.S...  60.1 us
    unnamed x33, local copies, waits for them, and re-layouts  17.2 us
    all_to_all x1, waiting for transfers between devices, on_device(): lax.all_to_all(grad_slab.reshape(c1, planes, rows, depth), 'gz', split_ax...  10.9 us
    all_to_all x1, starting transfers between devices, on_device(): lax.all_to_all(volume, 'gz', split_axis=1, concat_axis=3, tiled=True)  10.1 us
    all_to_all x1, starting transfers between devices, on_device(): lax.all_to_all(grad_slab.reshape(c1, planes, rows, depth), 'gz', split_ax...  6.33 us
    all_to_all x1, waiting for transfers between devices, on_device(): lax.all_to_all(volume, 'gz', split_axis=1, concat_axis=3, tiled=True)  2.68 us
  transfers between devices with their start and end apart: 2, of which 2 were waited for; matrix products, arithmetic and copies ran while one was open for 7% of the time, Pallas kernels for 0%

profile of v1, /device:TPU:1, one launch (start us, length us, event | category | flops | bytes accessed | tf_op | source)
XLA Modules:
  0.0 117.3 jit_solution(9705131833264169761)
XLA Ops:
  0.6 3.2 %copy.34 = bf16[32,32,8,16]{0,3,2,1:T(8,128)(2,1)S(1)} copy(bf16[32,32,8,16]{1,3,2,0:T(8,128)(2,1)} %param.6) | data formatting | bytes 524288 | tf_op args[0]
  3.9 1.7 %reshape.106 = bf16[16,2,4096]{2,1,0:T(2,128)(2,1)} reshape(bf16[32,8,16,32]{3,2,1,0:T(8,128)(2,1)S(1)} %bitcast.45) | data formatting | bytes 524288
  5.6 10.1 %all-to-all-start = ((bf16[16,2,4096]{2,1,0:T(2,128)(2,1)}), bf16[16,2,4096]{2,1,0:T(2,128)(2,1)S(1)}, u32[]{:S(2)}, u32[]{:S(2)}) async-start(bf16[16,2,4096]{2,1,0:T(2,128)(2,1)} %reshape.106), calls=%async_computation | async-start | bytes 524288 | tf_op jit(solution)/shard_map/all_to_all | solution.py:421
  15.7 0.3 copy.38
  16.0 0.9 copy.55
  17.1 0.9 reshape.99.refs_9_
  18.0 1.0 copy.37
  19.0 0.7 copy.57
  19.7 0.8 copy.36
  20.4 0.7 copy-done.6
  21.1 0.7 copy.42.refs_5_
  21.8 0.7 copy-done.7
  22.5 0.7 copy.41.refs_2_
  23.2 0.6 convert_convert_fusion.refs_8_
  23.8 0.8 fusion.refs_3_
  24.6 2.7 %all-to-all-done = bf16[16,2,4096]{2,1,0:T(2,128)(2,1)S(1)} async-done(((bf16[16,2,4096]{2,1,0:T(2,128)(2,1)}), bf16[16,2,4096]{2,1,0:T(2,128)(2,1)S(1)}, u32[]{:S(2)}, u32[]{:S(2)}) %all-to-all-start) | async-done | bytes 262176 | tf_op jit(solution)/shard_map/all_to_all | solution.py:421
  27.3 0.5 reshape.107
  28.0 1.0 copy.40.refs_0_
  29.0 60.1 %shard_map.109 = (bf16[128,512]{1,0:T(8,128)(2,1)}, bf16[32,4096]{1,0:T(8,128)(2,1)}, f32[864,64]{1,0:T(8,128)}, f32[1,64]{1,0:T(1,128)}, f32[1728,128]{1,0:T(8,128)}, /*index=5*/f32[1,128]{1,0:T(1,128)}) custom-call(bf16[32,4096]{1,0:T(8,128)(2,1)} %copy.40.refs_0_, bf16[64,864]{1,0:T(8,128)(2,1)} %bitcast.58, f32[64,1]{1,0:T(8,128)} %copy.41.refs_2_, ...), custom_call_target="tpu_custom_call" | custom-call | tf_op jit(solution)/shard_map/pallas_call | solution.py:365
  89.1 1.0 copy.51
  90.1 1.0 copy.43
  91.2 1.7 %reshape.108 = bf16[16,2,4096]{2,1,0:T(2,128)(2,1)} reshape(bf16[256,2,8,32]{3,2,1,0:T(8,128)(2,1)S(1)} %bitcast.41) | data formatting | bytes 524288
  92.9 6.3 %all-to-all-start.1 = ((bf16[16,2,4096]{2,1,0:T(2,128)(2,1)}), bf16[16,2,4096]{2,1,0:T(2,128)(2,1)S(1)}, u32[]{:S(2)}, u32[]{:S(2)}) async-start(bf16[16,2,4096]{2,1,0:T(2,128)(2,1)} %reshape.108), calls=%async_computation.1 | async-start | bytes 524288 | tf_op jit(solution)/shard_map/all_to_all | solution.py:434
  99.2 0.7 reshape.100
  99.9 10.9 %all-to-all-done.1 = bf16[16,2,4096]{2,1,0:T(2,128)(2,1)S(1)} async-done(((bf16[16,2,4096]{2,1,0:T(2,128)(2,1)}), bf16[16,2,4096]{2,1,0:T(2,128)(2,1)S(1)}, u32[]{:S(2)}, u32[]{:S(2)}) %all-to-all-start.1) | async-done | bytes 262176 | tf_op jit(solution)/shard_map/all_to_all | solution.py:434
  110.8 0.5 reshape.109
  111.3 0.3 copy.45
  111.6 2.9 %copy.47 = bf16[32,32,8,16]{1,3,2,0:T(8,128)(2,1)} copy(bf16[32,32,8,16]{0,3,2,1:T(8,128)(2,1)S(1)} %bitcast.46) | data formatting | bytes 524288
  114.5 0.8 copy.62
  115.3 0.5 copy.63
  115.8 0.9 copy.64
  116.7 0.5 copy.65
  (23 shorter events, 0.5 us)
Async XLA Ops:
  5.6 10.1 %copy-start = (bf16[3,3,3,64,128]{4,3,2,1,0:T(8,128)(2,1)S(1)}, bf16[3,3,3,64,128]{4,3,2,1,0:T(8,128)(2,1)}, u32[]{:S(2)}) copy-start(bf16[3,3,3,64,128]{4,3,2,1,0:T(8,128)(2,1)} %param.9) | copy-start | bytes 1327108
  5.6 21.7 %all-to-all-start = ((bf16[16,2,4096]{2,1,0:T(2,128)(2,1)}), bf16[16,2,4096]{2,1,0:T(2,128)(2,1)S(1)}, u32[]{:S(2)}, u32[]{:S(2)}) async-start(bf16[16,2,4096]{2,1,0:T(2,128)(2,1)} %reshape.106), calls=%async_computation | async-start | bytes 524288 | tf_op jit(solution)/shard_map/all_to_all | solution.py:421
  16.0 1.0 copy-start.2
  18.0 1.0 copy-start.4
  20.4 0.7 copy-start.6
  21.8 0.7 copy-start.7
  92.9 6.3 %copy-start.5 = (bf16[128,512]{1,0:T(8,128)(2,1)S(1)}, bf16[128,512]{1,0:T(8,128)(2,1)}, u32[]{:S(2)}) copy-start(bf16[128,512]{1,0:T(8,128)(2,1)} %get-tuple-element.12) | copy-start | bytes 393220
  92.9 17.9 %all-to-all-start.1 = ((bf16[16,2,4096]{2,1,0:T(2,128)(2,1)}), bf16[16,2,4096]{2,1,0:T(2,128)(2,1)S(1)}, u32[]{:S(2)}, u32[]{:S(2)}) async-start(bf16[16,2,4096]{2,1,0:T(2,128)(2,1)} %reshape.108), calls=%async_computation.1 | async-start | bytes 524288 | tf_op jit(solution)/shard_map/all_to_all | solution.py:434
  111.6 2.9 %copy-start.3 = (f32[864,64]{1,0:T(8,128)S(1)}, f32[864,64]{1,0:T(8,128)}, u32[]{:S(2)}) copy-start(f32[864,64]{1,0:T(8,128)} %get-tuple-element.14) | copy-start | bytes 663556
  114.5 1.3 %copy-start.1 = (f32[1728,128]{1,0:T(8,128)S(1)}, f32[1728,128]{1,0:T(8,128)}, u32[]{:S(2)}) copy-start(f32[1728,128]{1,0:T(8,128)} %get-tuple-element.16) | copy-start | bytes 2654212
  114.5 0.8 copy-start.9
  115.8 0.9 copy-start.8

commit v2 on v1

v2 whole, which is shorter than its diff:
```python
import functools
import math

import jax
import jax.numpy as jnp
from jax import lax
from jax.experimental import pallas as pl
from jax.experimental.pallas import tpu as pltpu
from jax.sharding import PartitionSpec as P

MESH = pl.DeviceIdType.MESH
LANES = 128
BOTH = (0, 1)
NEAR = (-1, 0, 1)


def slope_of(value):
    sigma = jax.nn.sigmoid(value)
    return sigma + value * sigma * (1.0 - sigma)


def dot(left, right):
    return jnp.dot(left, right, preferred_element_type=jnp.float32)


def dot_rows(left, right):
    return lax.dot_general(
        left, right, (((1,), (1,)), ((), ())), preferred_element_type=jnp.float32
    )


def roll(value, by):
    by = by % LANES
    return pltpu.roll(value, by, 1) if by else value


def lanes_at(index, count=1):
    begin = index * LANES
    if not isinstance(begin, int):
        begin = pl.multiple_of(begin, LANES)
    return pl.ds(begin, count * LANES)


def within(at, count):
    return (at >= 0) & (at < count)


class Grid:
    def __init__(self, nx, ny, nz):
        self.ny, self.nz = ny, nz
        self.plane = ny * nz
        self.fold = LANES // self.plane
        self.tiles = nx // self.fold
        self.zpacks = -(-self.tiles // nz)
        self.ypacks = -(-self.tiles // ny)
        self.group = max(ny, min(nz, self.tiles))

    def at(self, rows):
        lane = lax.broadcasted_iota(jnp.int32, (rows, LANES), 1)
        return lane // self.plane, lane // self.nz % self.ny, lane % self.nz

    def corner_groups(self, channels):
        return min(channels // 16, self.nz // self.ypacks)


class Exchange:
    def __init__(self, grid, channels, buffers, sems, at):
        self.grid, self.channels = grid, channels
        self.zs, self.zr, self.ys, self.yr, self.cs, self.cr, self.xs, self.xr = buffers
        self.gx, self.gy, self.gz = [lax.axis_index(axis) for axis in ("gx", "gy", "gz")]
        cuts_y, cuts_z = lax.axis_size("gy"), lax.axis_size("gz")
        moves = []
        step = (1, -1)
        for side in BOTH:
            moves.append((self.ys.at[side], self.yr.at[side], 0, step[side], 0))
        for dy in NEAR:
            for dz in NEAR:
                moves.append((self.xs, self.xr.at[(1 - dy) * 3 + 1 - dz], 1, dy, dz))
        for side in BOTH:
            moves.append((self.zs.at[side], self.zr.at[side], 0, 0, step[side]))
        for sy in BOTH:
            for sz in BOTH:
                i = sy * 2 + sz
                moves.append((self.cs.at[i], self.cr.at[i], 0, step[sy], step[sz]))
        self.moves = []
        for i, (source, target, across, dy, dz) in enumerate(moves):
            copy = pltpu.make_async_remote_copy(
                src_ref=source,
                dst_ref=target,
                send_sem=sems.at[0, at, i],
                recv_sem=sems.at[1, at, i],
                device_id={
                    "gx": (self.gx + across) % 2,
                    "gy": (self.gy + dy + cuts_y) % cuts_y,
                    "gz": (self.gz + dz + cuts_z) % cuts_z,
                },
                device_id_type=MESH,
            )
            goes = within(self.gy + dy, cuts_y) & within(self.gz + dz, cuts_z)
            comes = within(self.gy - dy, cuts_y) & within(self.gz - dz, cuts_z)
            self.moves.append((copy, goes, comes))

    def clear(self):
        for ref in (self.zr, self.yr, self.cr, self.xr):
            ref[...] = jnp.zeros_like(ref)

    def pack(self, field):
        grid, c = self.grid, self.channels
        spot, y, z = grid.at(c)
        last_z, last_y = grid.nz - 1, grid.ny - 1
        ends = [field[:, lanes_at(t)] for t in (grid.tiles - 1, 0)]
        if grid.fold == 1:
            self.xs[...] = jnp.where(spot + self.gx == 0, *ends)
        else:
            part = c // grid.fold
            place = grid.at(part)[0]
            made = []
            for end, i in zip(ends, (grid.fold - 1, 0)):
                out = end[:part]
                out = roll(out, grid.plane * -i)
                for j in range(1, grid.fold):
                    piece = roll(end[j * part : (j + 1) * part], grid.plane * (j - i))
                    out = jnp.where(place == j, piece, out)
                made.append(out)
            self.xs[...] = jnp.where(place * 0 + self.gx == 0, *made)

        def one(q, carry):
            held = [None, None]
            rows = [None, None]
            for k in range(grid.group):
                tile = field[:, lanes_at(q * grid.group + k)]
                j = k % grid.ny
                for side in BOTH:
                    piece = roll(tile, k - last_z if side == 0 else k)
                    held[side] = piece if k == 0 else jnp.where(z == k, piece, held[side])
                    piece = roll(tile, grid.nz * (j - last_y if side == 0 else j))
                    rows[side] = piece if j == 0 else jnp.where(y == j, piece, rows[side])
                    if j == last_y:
                        self.ys[side, :, lanes_at(q * (grid.group // grid.ny) + k // grid.ny)] = rows[side]
            for side in BOTH:
                self.zs[side, :, lanes_at(q)] = held[side]
            return carry

        loops = grid.tiles // grid.group
        if loops == 1:
            one(0, 0)
        else:
            lax.fori_loop(0, loops, one, 0)
        groups, packs = grid.corner_groups(c), grid.ypacks
        part = c // groups
        z = grid.at(part)[2]
        for sy in BOTH:
            for sz in BOTH:
                out = None
                for j in range(groups):
                    for p in range(packs):
                        to = packs * j + p
                        piece = self.ys[sy, j * part : (j + 1) * part, lanes_at(p)]
                        piece = roll(piece, to - (last_z if sz == 0 else 0))
                        out = piece if out is None else jnp.where(z == to, piece, out)
                self.cs[sy * 2 + sz] = out

    def start(self):
        for copy, goes, _ in self.moves:
            pl.when(goes)(copy.start)

    def wait(self):
        for copy, goes, comes in self.moves:
            pl.when(goes)(copy.wait_send)
            pl.when(comes)(copy.wait_recv)

    def shift_z(self, tile, low, high, dz, z):
        if dz == 0:
            return tile
        if dz < 0:
            return jnp.where(z == 0, low, roll(tile, 1))
        return jnp.where(z == self.grid.nz - 1, high, roll(tile, -1))

    def shift_y(self, tile, low, high, dy, y):
        if dy == 0:
            return tile
        if dy < 0:
            return jnp.where(y == 0, low, roll(tile, self.grid.nz))
        return jnp.where(y == self.grid.ny - 1, high, roll(tile, -self.grid.nz))

    def beyond(self):
        grid, c = self.grid, self.channels
        _, y, z = grid.at(c)
        if grid.fold == 1:
            came = [self.xr[i] for i in range(9)]
        else:
            last = grid.fold - 1
            came = [
                jnp.concatenate([roll(self.xr[i], grid.plane * (last - j)) for j in range(grid.fold)], axis=0)
                for i in range(9)
            ]
        along = grid.nz * (grid.ny - 1)
        rows = []
        for dy in range(3):
            low, here, high = came[dy * 3 : dy * 3 + 3]
            low, high = roll(low, 1 - grid.nz), roll(high, grid.nz - 1)
            rows.append([self.shift_z(here, low, high, dz, z) for dz in NEAR])
        return [
            self.shift_y(rows[1][dz], roll(rows[0][dz], -along), roll(rows[2][dz], along), dy, y)
            for dy in NEAR
            for dz in range(3)
        ]

    def strips(self, shifted):
        grid, c = self.grid, self.channels
        groups, packs = grid.corner_groups(c), grid.ypacks
        _, _, z = grid.at(c)
        for side in BOTH:
            for p in range(packs):
                tile = self.yr[side, :, lanes_at(p)]
                ends = []
                for sz in BOTH:
                    to = 0 if sz == 0 else grid.nz - 1
                    corner = self.cr[side * 2 + sz]
                    ends.append(
                        jnp.concatenate([roll(corner, to - packs * j - p) for j in range(groups)], axis=0)
                    )
                for dz in NEAR:
                    shifted[side * 3 + dz + 1, :, lanes_at(p)] = self.shift_z(tile, *ends, dz, z)

    def tile_shifts(self, field, shifted, q, k):
        grid, c = self.grid, self.channels
        _, y, z = grid.at(c)
        last_z, last_y = grid.nz - 1, grid.ny - 1
        tile = field[:, lanes_at(q * grid.group + k)]
        low = roll(self.zr[0, :, lanes_at(q)], -k)
        high = roll(self.zr[1, :, lanes_at(q)], last_z - k)
        moved = [self.shift_z(tile, low, high, dz, z) for dz in NEAR]
        p, j = q * (grid.group // grid.ny) + k // grid.ny, k % grid.ny
        out = []
        for dy in NEAR:
            for dz in range(3):
                low = high = None
                if dy < 0:
                    low = roll(shifted[dz, :, lanes_at(p)], -grid.nz * j)
                if dy > 0:
                    high = roll(shifted[3 + dz, :, lanes_at(p)], grid.nz * (last_y - j))
                out.append(self.shift_y(moved[dz], low, high, dy, y))
        return out

    def only(self, value, side):
        flag = lax.broadcasted_iota(jnp.int32, value.shape, 1) * 0 + self.gx
        return jnp.where(flag == side, value, jnp.zeros_like(value))

    def fine_windows(self, field, shifted, windows):
        grid, c = self.grid, self.channels
        self.strips(shifted)
        for i, value in enumerate(self.beyond()):
            windows[i * c : (i + 1) * c, lanes_at(0)] = self.only(value, 1)
            windows[i * c : (i + 1) * c, lanes_at(grid.tiles + 1)] = self.only(value, 0)

        def one(q, carry):
            for k in range(grid.group):
                for i, value in enumerate(self.tile_shifts(field, shifted, q, k)):
                    windows[i * c : (i + 1) * c, lanes_at(q * grid.group + k + 1)] = value
            return carry

        lax.fori_loop(0, grid.tiles // grid.group, one, 0)

    def coarse_windows(self, field, shifted, windows):
        grid, c = self.grid, self.channels
        spot = grid.at(c)[0]
        self.strips(shifted)
        outer = self.beyond()
        tiles = [self.tile_shifts(field, shifted, 0, k) for k in range(grid.tiles)]
        for i in range(9):
            low = roll(self.only(outer[i], 1), grid.plane)
            high = self.only(outer[i], 0)
            rows = [slice((dx * 9 + i) * c, (dx * 9 + i + 1) * c) for dx in range(3)]
            up = [roll(tile[i], grid.plane) for tile in tiles]
            down = [roll(tile[i], -grid.plane) for tile in tiles]
            for t in range(grid.tiles):
                before = up[t - 1] if t else low
                after = down[t + 1] if t + 1 < grid.tiles else high
                windows[rows[0], lanes_at(t)] = jnp.where(spot == 0, before, up[t])
                windows[rows[1], lanes_at(t)] = tiles[t][i]
                windows[rows[2], lanes_at(t)] = jnp.where(spot == grid.fold - 1, after, down[t])


class Summing:
    def __init__(self, acc, stage, first, mine, second, whole, sems):
        self.acc, self.stage, self.first = acc, stage, first
        self.mine, self.second, self.whole = mine, second, whole
        self.sems = sems
        gy = lax.axis_size("gy")
        self.count = lax.axis_size("gx") * gy
        self.depth = lax.axis_size("gz")
        self.me = lax.axis_index("gx") * gy + lax.axis_index("gy")
        self.level = lax.axis_index("gz")

    def across(self, phase, k, source, target):
        gy = lax.axis_size("gy")
        to = (self.me + k) % self.count
        return pltpu.make_async_remote_copy(
            src_ref=source(to),
            dst_ref=target,
            send_sem=self.sems.at[phase, 0, k],
            recv_sem=self.sems.at[phase, 1, k],
            device_id={"gx": to // gy, "gy": to % gy},
            device_id_type=MESH,
        )

    def along(self, k):
        return pltpu.make_async_remote_copy(
            src_ref=self.mine,
            dst_ref=self.second.at[self.level],
            send_sem=self.sems.at[1, 0, k],
            recv_sem=self.sems.at[1, 1, k],
            device_id={"gz": (self.level + k) % self.depth},
            device_id_type=MESH,
        )

    def scatters(self):
        return [
            self.across(0, k, lambda to: self.stage.at[to], self.first.at[self.me])
            for k in range(1, self.count)
        ]

    def alongs(self):
        return [self.along(k) for k in range(1, self.depth)]

    def gathers(self):
        here = self.whole.at[self.me]
        return [self.across(2, k, lambda to: here, here) for k in range(1, self.count)]

    def start(self):
        chunk = self.stage.shape[1]
        for i in range(self.count):
            self.stage[i] = self.acc[i * chunk : (i + 1) * chunk].astype(jnp.bfloat16)
        for copy in self.scatters():
            copy.start()
        self.first[self.me] = self.stage[self.me]

    def total(self, parts):
        total = parts[0].astype(jnp.float32)
        for i in range(1, parts.shape[0]):
            total = total + parts[i].astype(jnp.float32)
        return total.astype(jnp.bfloat16)

    def middle(self):
        for copy in self.scatters():
            copy.wait()
        part = self.total(self.first)
        self.mine[...] = part
        for copy in self.alongs():
            copy.start()
        self.second[self.level] = part

    def last(self):
        for copy in self.alongs():
            copy.wait()
        self.whole[self.me] = self.total(self.second)
        for copy in self.gathers():
            copy.start()

    def finish(self):
        for copy in self.gathers():
            copy.wait()


class Slabs:
    def __init__(self, sent, came, sems, grid):
        self.sent, self.came, self.sems, self.grid = sent, came, sems, grid
        self.depth, self.level = lax.axis_size("gz"), lax.axis_index("gz")

    def copies(self):
        out = []
        for k in range(1, self.depth):
            to = (self.level + k) % self.depth
            out.append(
                pltpu.make_async_remote_copy(
                    src_ref=self.sent.at[to],
                    dst_ref=self.came.at[self.level],
                    send_sem=self.sems.at[0, k],
                    recv_sem=self.sems.at[1, k],
                    device_id={"gz": to},
                    device_id_type=MESH,
                )
            )
        return out

    def pack(self, field):
        fold, plane = self.grid.fold, self.grid.plane
        part = self.sent.shape[1]
        spot = self.grid.at(part)[0]
        for t in range(self.grid.tiles):
            for i in range(fold):
                out = None
                for j in range(fold):
                    piece = roll(field[j * part : (j + 1) * part, lanes_at(t)], plane * (j - i))
                    out = piece if out is None else jnp.where(spot == j, piece, out)
                self.sent[t * fold + i] = out
        for copy in self.copies():
            copy.start()
        self.came[self.level] = self.sent[self.level]

    def unpack(self, field):
        for copy in self.copies():
            copy.wait()
        fold, plane = self.grid.fold, self.grid.plane
        part = self.came.shape[1]
        spot = self.grid.at(part)[0]
        for t in range(self.grid.tiles):
            for j in range(fold):
                out = None
                for i in range(fold):
                    piece = roll(self.came[t * fold + i], plane * (i - j))
                    out = piece if out is None else jnp.where(spot == i, piece, out)
                field[j * part : (j + 1) * part, lanes_at(t)] = out


def greet():
    gx, gy, gz = [lax.axis_size(axis) for axis in ("gx", "gy", "gz")]
    me = lax.axis_index("gx") * gy + lax.axis_index("gy")
    level, row, half = lax.axis_index("gz"), lax.axis_index("gy"), lax.axis_index("gx")
    barrier = pltpu.get_barrier_semaphore()
    signal = lambda device: pl.semaphore_signal(barrier, inc=1, device_id=device, device_id_type=MESH)
    for k in range(1, gx * gy):
        to = (me + k) % (gx * gy)
        signal({"gx": to // gy, "gy": to % gy})
    for k in range(1, gz):
        signal({"gz": (level + k) % gz})
    extra = 0
    for across in BOTH:
        for dy in NEAR:
            for dz in NEAR:
                if dz and (across or dy):
                    extra += 1
                    signal(
                        {
                            "gx": (half + across) % gx,
                            "gy": (row + dy + gy) % gy,
                            "gz": (level + dz + gz) % gz,
                        }
                    )
    return barrier, gx * gy + gz - 2 + extra


def spread_map(fine, coarse):
    shape = (LANES, coarse.fold * LANES)
    small = lax.broadcasted_iota(jnp.int32, shape, 0)
    large = lax.broadcasted_iota(jnp.int32, shape, 1)
    y, z = large % LANES // fine.nz, large % fine.nz
    match = (
        (small // coarse.plane == large // LANES)
        & (small // coarse.nz % coarse.ny == y // 2)
        & (small % coarse.nz == z // 2)
    )
    ones = match.astype(jnp.float32)
    first = (match & (y % 2 == 0) & (z % 2 == 0)).astype(jnp.float32)
    return ones.astype(jnp.bfloat16), first.astype(jnp.bfloat16)


def order_map(coarse, count):
    shape = (coarse.plane * count,) * 2
    row = lax.broadcasted_iota(jnp.int32, shape, 0)
    column = lax.broadcasted_iota(jnp.int32, shape, 1)
    wide = count * coarse.nz
    match = (
        (row // wide == column // coarse.nz % coarse.ny)
        & (row % wide // coarse.nz == column // coarse.plane)
        & (row % coarse.nz == column % coarse.nz)
    )
    return match.astype(jnp.float32).astype(jnp.bfloat16)


def column_of(row):
    size = row.shape[1]
    across = lax.broadcasted_iota(jnp.int32, (size, size), 0)
    down = lax.broadcasted_iota(jnp.int32, (size, size), 1)
    return jnp.sum(jnp.where(across == down, row, 0.0), axis=1, keepdims=True)


def whole_kernel(setting, *refs):
    fine_size, coarse_size, scales, names = setting
    fine, coarse = Grid(*fine_size), Grid(*coarse_size)
    named = dict(zip(names, refs))
    r = lambda name: named[name]
    fields = ("a", "b", "gb", "ga")
    grids = (fine, coarse, coarse, fine)
    volume, w_a, b_a, w_b, b_b, cot = [r(n) for n in ("volume", "w_a", "b_a", "w_b", "b_b", "cot")]
    features, grad_in, out_wa, out_ba, out_wb, out_bb = [
        r(n) for n in ("features", "grad_in", "out_wa", "out_ba", "out_wb", "out_bb")
    ]
    c1, c2, c3 = volume.shape[0], w_a.shape[1], w_b.shape[1]
    widths = dict(zip(fields, (c1, c2, c3, c2)))
    halos = {
        name: Exchange(
            grid,
            widths[name],
            [r(name + part) for part in ("_zs", "_zr", "_ys", "_yr", "_cs", "_cr", "_xs", "_xr")],
            r("halo_sems"),
            i,
        )
        for i, (name, grid) in enumerate(zip(fields, grids))
    }
    strips = {name: r(name + "_strips") for name in fields}
    win_a, win_b, win_gb, win_ga = [r(name + "_win") for name in fields]
    before_a, pooled, grad_b, grad_a = [r(n) for n in ("before_a", "pooled", "grad_b", "grad_a")]
    acc_a, acc_b, mixed, feat = [r(n) for n in ("acc_a", "acc_b", "mixed", "feat")]
    sum_a = Summing(acc_a, *[r(f"sum_a{i}") for i in range(5)], r("sum_sems").at[0])
    sum_b = Summing(acc_b, *[r(f"sum_b{i}") for i in range(5)], r("sum_sems").at[1])
    cots = Slabs(r("cot_sent"), r("cot_came"), r("slab_sems").at[0], coarse)
    feats = Slabs(r("feat_sent"), r("feat_came"), r("slab_sems").at[1], coarse)
    out_a, in_a, out_b, in_b, spread, thin, order = [
        r(n) for n in ("to_a", "from_a", "to_b", "from_b", "spread", "thin", "order")
    ]
    bf16 = jnp.bfloat16

    for name in fields:
        halos[name].clear()
    barrier, arrivals = greet()
    halos["a"].pack(volume)
    order[...] = order_map(coarse, lax.axis_size("gz"))
    mixed[...] = dot(cot[...], order[...]).astype(bf16)
    pl.semaphore_wait(barrier, arrivals)
    halos["a"].start()
    cots.pack(mixed)

    taps = 9
    for dx in range(3):
        out_a[dx] = w_a[dx * taps * c1 : (dx + 1) * taps * c1].T
        for k in range(taps):
            tap = 26 - dx * taps - k
            in_a[dx, :, k * c2 : (k + 1) * c2] = w_a[tap * c1 : (tap + 1) * c1]
    out_b[...] = w_b[...].T
    for k in range(27):
        in_b[:, k * c3 : (k + 1) * c3] = w_b[(26 - k) * c2 : (27 - k) * c2]
    wide, narrow = spread_map(fine, coarse)
    spread[...] = wide
    thin[...] = narrow
    bias_a, bias_b = column_of(b_a[...]), column_of(b_b[...])
    acc_a[...] = jnp.zeros_like(acc_a)
    acc_b[...] = jnp.zeros_like(acc_b)

    halos["a"].wait()
    halos["a"].fine_windows(volume, strips["a"], win_a)
    many = 2 * coarse.fold

    def forward_a(g, carry):
        before = bias_a
        for dx in range(3):
            before = before + dot(out_a[dx], win_a[:, lanes_at(g * many + dx, many)])
        before_a[:, lanes_at(g * many, many)] = before
        active = before * jax.nn.sigmoid(before)
        pieces = []
        for i in range(coarse.fold):
            first = active[:, 2 * i * LANES : (2 * i + 1) * LANES]
            pair = first + active[:, (2 * i + 1) * LANES : (2 * i + 2) * LANES]
            pair = pair + roll(pair, -1)
            pair = pair + roll(pair, -fine.nz)
            pieces.append((pair * 0.125).astype(bf16))
        pooled[:, lanes_at(g)] = dot_rows(jnp.concatenate(pieces, axis=1), thin[...]).astype(bf16)
        return carry

    lax.fori_loop(0, coarse.tiles, forward_a, 0)
    halos["b"].pack(pooled)
    halos["b"].start()
    cots.unpack(mixed)
    halos["b"].wait()
    halos["b"].coarse_windows(pooled, strips["b"], win_b)
    before = dot(out_b[...], win_b[...]) + bias_b
    grad_b[...] = (mixed[...].astype(jnp.float32) * slope_of(before)).astype(bf16)
    halos["gb"].pack(grad_b)
    halos["gb"].start()
    feat[...] = (before * jax.nn.sigmoid(before)).astype(bf16)
    feats.pack(feat)
    top_b = out_wb.shape[0]
    grad = grad_b[...]
    acc_b[:top_b] = dot_rows(win_b[...], grad)
    acc_b[top_b : top_b + 8] = dot_rows(jnp.ones((8, grad.shape[1]), bf16), grad)
    sum_b.start()
    halos["gb"].wait()
    halos["gb"].coarse_windows(grad_b, strips["gb"], win_gb)
    pooled[...] = dot(in_b[...], win_gb[...]).astype(bf16)

    def backward_b(g, carry):
        wide = dot(pooled[:, lanes_at(g)], spread[...]) * 0.125
        for i in range(coarse.fold):
            for j in BOTH:
                here = lanes_at(g * many + 2 * i + j)
                slope = slope_of(before_a[:, here])
                grad_a[:, here] = (wide[:, i * LANES : (i + 1) * LANES] * slope).astype(bf16)
        return carry

    lax.fori_loop(0, coarse.tiles, backward_b, 0)
    halos["ga"].pack(grad_a)
    halos["ga"].start()
    grad = grad_a[...]
    half, width = out_wa.shape[0] // 2, out_wa.shape[1]
    parts = [dot_rows(win_a[:, lanes_at(dx, fine.tiles)], grad) for dx in range(3)]
    whole = jnp.concatenate(parts, axis=0)
    acc_a[:half, :width] = whole[:half]
    acc_a[:half, width:] = whole[half:]
    acc_a[half : half + 8, :width] = dot_rows(jnp.ones((8, grad.shape[1]), bf16), grad)
    sum_a.start()
    sum_b.middle()
    halos["ga"].wait()
    halos["ga"].fine_windows(grad_a, strips["ga"], win_ga)

    def backward_a(g, carry):
        total = dot(in_a[0], win_ga[:, lanes_at(g * many, many)])
        for dx in (1, 2):
            total = total + dot(in_a[dx], win_ga[:, lanes_at(g * many + dx, many)])
        grad_in[:, lanes_at(g * many, many)] = total.astype(bf16)
        return carry

    lax.fori_loop(0, coarse.tiles, backward_a, 0)
    sum_a.middle()
    feats.unpack(feat)
    features[...] = dot_rows(feat[...], order[...]).astype(bf16)
    sum_b.last()
    sum_a.last()
    sum_b.finish()
    all_a, all_b = r("sum_a4"), r("sum_b4")
    scale_a, scale_b = scales
    flat_b = all_b[...].astype(jnp.float32).reshape(-1, all_b.shape[2]) * scale_b
    out_wb[...] = flat_b[:top_b]
    out_bb[...] = flat_b[top_b : top_b + 1]
    sum_a.finish()
    flat_a = all_a[...].astype(jnp.float32).reshape(-1, all_a.shape[2]) * scale_a
    out_wa[:half] = flat_a[:half, :width]
    out_wa[half:] = flat_a[:half, width:]
    out_ba[...] = flat_a[half : half + 1, :width]


def on_device(volume, weight_a, bias_a, weight_b, bias_b, cotangent):
    f32, bf16 = jnp.float32, jnp.bfloat16
    members, levels = lax.axis_size("gx") * lax.axis_size("gy"), lax.axis_size("gz")
    c1, nx, ny, nz = volume.shape
    c2, c3 = weight_b.shape[3:]
    cells = nx * ny * nz
    fewer = cells // 8
    scale_a = 1.0 / math.sqrt(cells * members * levels)
    scale_b = 1.0 / math.sqrt(cells * members * levels // 8)
    fine_size, coarse_size = (nx, ny, nz), (nx // 2, ny // 2, nz // 2)
    fine, coarse = Grid(*fine_size), Grid(*coarse_size)
    rows_a = 27 * c1 // 2 + 16
    rows_a += -rows_a % (16 * members)
    rows_b = 27 * c2 + 16
    rows_b += -rows_b % (16 * members)
    operands = {
        "volume": volume.reshape(c1, cells),
        "w_a": weight_a.reshape(27 * c1, c2),
        "b_a": bias_a.reshape(1, c2),
        "w_b": weight_b.reshape(27 * c2, c3),
        "b_b": bias_b.reshape(1, c3),
        "cot": cotangent.reshape(c3, fewer),
    }
    outs = {
        "features": ((c3, fewer), bf16),
        "grad_in": ((c1, cells), bf16),
        "out_wa": ((27 * c1, c2), f32),
        "out_ba": ((1, c2), f32),
        "out_wb": ((27 * c2, c3), f32),
        "out_bb": ((1, c3), f32),
    }
    scratch = {}
    for name, grid, c in (("a", fine, c1), ("b", coarse, c2), ("gb", coarse, c3), ("ga", fine, c2)):
        for end in ("s", "r"):
            scratch[f"{name}_z{end}"] = pltpu.VMEM((2, c, grid.zpacks * LANES), bf16)
            scratch[f"{name}_y{end}"] = pltpu.VMEM((2, c, grid.ypacks * LANES), bf16)
            scratch[f"{name}_c{end}"] = pltpu.VMEM((4, c // grid.corner_groups(c), LANES), bf16)
        scratch[f"{name}_xs"] = pltpu.VMEM((c // grid.fold, LANES), bf16)
        scratch[f"{name}_xr"] = pltpu.VMEM((9, c // grid.fold, LANES), bf16)
        scratch[f"{name}_strips"] = pltpu.VMEM((6, c, grid.ypacks * LANES), bf16)
        shape = (9 * c, (grid.tiles + 2) * LANES) if grid is fine else (27 * c, grid.tiles * LANES)
        scratch[f"{name}_win"] = pltpu.VMEM(shape, bf16)
    scratch["before_a"] = pltpu.VMEM((c2, cells), f32)
    scratch["pooled"] = pltpu.VMEM((c2, fewer), bf16)
    scratch["grad_b"] = pltpu.VMEM((c3, fewer), bf16)
    scratch["grad_a"] = pltpu.VMEM((c2, cells), bf16)
    scratch["mixed"] = pltpu.VMEM((c3, fewer), bf16)
    scratch["feat"] = pltpu.VMEM((c3, fewer), bf16)
    for name, rows in (("a", rows_a), ("b", rows_b)):
        chunk = rows // members
        scratch[f"acc_{name}"] = pltpu.VMEM((rows, LANES), f32)
        for i, shape in enumerate(
            ((members, chunk), (members, chunk), (chunk,), (levels, chunk), (members, chunk))
        ):
            scratch[f"sum_{name}{i}"] = pltpu.VMEM((*shape, LANES), bf16)
    for name in ("cot_sent", "cot_came", "feat_sent", "feat_came"):
        scratch[name] = pltpu.VMEM((levels, c3 // coarse.fold, LANES), bf16)
    scratch["to_a"] = pltpu.VMEM((3, c2, 9 * c1), bf16)
    scratch["from_a"] = pltpu.VMEM((3, c1, 9 * c2), bf16)
    scratch["to_b"] = pltpu.VMEM((c3, 27 * c2), bf16)
    scratch["from_b"] = pltpu.VMEM((c2, 27 * c3), bf16)
    scratch["spread"] = pltpu.VMEM((LANES, coarse.fold * LANES), bf16)
    scratch["thin"] = pltpu.VMEM((LANES, coarse.fold * LANES), bf16)
    scratch["order"] = pltpu.VMEM((fewer, fewer), bf16)
    scratch["halo_sems"] = pltpu.SemaphoreType.DMA((2, 4, 17))
    scratch["sum_sems"] = pltpu.SemaphoreType.DMA((2, 3, 2, max(members, levels)))
    scratch["slab_sems"] = pltpu.SemaphoreType.DMA((2, 2, levels))
    names = (*operands, *outs, *scratch)
    got = pl.pallas_call(
        functools.partial(whole_kernel, (fine_size, coarse_size, (scale_a, scale_b), names)),
        out_shape=[jax.ShapeDtypeStruct(shape, dtype) for shape, dtype in outs.values()],
        in_specs=[pl.BlockSpec(memory_space=pltpu.VMEM)] * len(operands),
        out_specs=[pl.BlockSpec(memory_space=pltpu.VMEM)] * len(outs),
        scratch_shapes=list(scratch.values()),
        compiler_params=pltpu.CompilerParams(
            collective_id=1, has_side_effects=True, vmem_limit_bytes=60 * 2**20
        ),
    )(*operands.values())
    features, grad_in, sum_wa, sum_ba, sum_wb, sum_bb = got
    return (
        features.reshape(cotangent.shape),
        grad_in.reshape(volume.shape),
        sum_wa.reshape(weight_a.shape),
        sum_ba.reshape(c2),
        sum_wb.reshape(weight_b.shape),
        sum_bb.reshape(c3),
    )


def solution(mesh):
    return jax.shard_map(
        on_device,
        mesh=mesh,
        in_specs=(P(None, "gx", "gy", "gz"), P(), P(), P(), P(), P(None, ("gx", "gz"), "gy", None)),
        out_specs=(
            P(None, ("gx", "gz"), "gy", None),
            P(None, "gx", "gy", "gz"),
            P(),
            P(),
            P(),
            P(),
        ),
        check_vma=False,
    )
```

time: 118 us -> 88.5 us (0.75)
  starting transfers between devices: 16.4 us -> 0 us
  Pallas kernels: 60.1 us -> 74 us
  waiting for transfers between devices: 13.6 us -> 0 us
  local copies, waits for them, and re-layouts: 25 us -> 13.6 us
  other arithmetic: 1.4 us -> 0 us
    all_to_all x2 -> x0, starting transfers between devices: 16.4 us -> none  [the longest x1 10.1 us: on_device(): lax.all_to_all(volume, 'gz', split_axis=1, concat_axis=3, tiled=True)]
    pallas_call x1, Pallas kernels: 60.1 us -> 74 us  [on_device(): pl.pallas_call(functools.partial(whole_kernel, (fine_size, coarse_size, (...]
    all_to_all x2 -> x0, waiting for transfers between devices: 13.6 us -> none  [the longest x1 10.9 us: on_device(): lax.all_to_all(grad_slab.reshape(c1, planes, rows, depth), 'gz', split_ax...]
    unnamed x33 -> x17, local copies, waits for them, and re-layouts: 17.2 us -> 10.5 us
    reshape x7 -> x1, local copies, waits for them, and re-layouts: 5.13 us -> 1.03 us  [on_device(): volume.reshape(c1, cells)]
    broadcast_in_dim x2 -> x0, local copies, waits for them, and re-layouts: 1.43 us -> none  [the longest x1 0.74 us: between_exchanges(): bias_b[:, None]]
    convert_element_type x2 -> x0, other arithmetic: 1.4 us -> none  [the longest x1 0.76 us: on_device(): (jnp.arange(depth)[:, None] // 2 == jnp.arange(depth // 2)[None]).astype(...]
  transfers between devices with their start and end apart: 2 -> 0, of which waited for: 2 -> 0; matrix products, arithmetic and copies ran while one was open for 7% -> 0% of each run, Pallas kernels for 0% -> 0%
where the time goes in v2:
time: 88.5 us; the launch traced here: 88.3 us
  Pallas kernels  74 us (84%)
  local copies, waits for them, and re-layouts  13.6 us (15%)
    pallas_call x1, Pallas kernels, on_device(): pl.pallas_call(functools.partial(whole_kernel, (fine_size, coarse_size, (...  74 us
    unnamed x17, local copies, waits for them, and re-layouts  10.5 us

profile of v2, /device:TPU:1, one launch (start us, length us, event | category | flops | bytes accessed | tf_op | source)
XLA Modules:
  0.0 88.3 jit_solution(3147480404216786463)
XLA Ops:
  0.6 1.6 %copy.22 = bf16[16,8,4,128]{3,1,2,0:T(8,128)(2,1)} copy(bf16[16,8,4,128]{3,2,1,0:T(4,128)(2,1)} %bitcast.23) | data formatting | bytes 262144
  2.2 3.2 %copy.15 = bf16[32,32,8,16]{0,3,2,1:T(8,128)(2,1)S(1)} copy(bf16[32,32,8,16]{1,3,2,0:T(8,128)(2,1)} %param.6) | data formatting | bytes 524288 | tf_op args[0]
  5.4 1.0 %copy.16.refs_0_ = bf16[32,4096]{1,0:T(8,128)(2,1)} copy(bf16[32,4096]{0,1:T(8,128)(2,1)S(1)} %bitcast.17) | data formatting | bytes 524288 | tf_op jit(solution)/shard_map/reshape | solution.py:648
  6.5 74.0 %shard_map.109 = (bf16[128,512]{1,0:T(8,128)(2,1)}, bf16[32,4096]{1,0:T(8,128)(2,1)}, f32[864,64]{1,0:T(8,128)}, f32[1,64]{1,0:T(1,128)}, f32[1728,128]{1,0:T(8,128)}, /*index=5*/f32[1,128]{1,0:T(1,128)}) custom-call(bf16[32,4096]{1,0:T(8,128)(2,1)} %copy.16.refs_0_, bf16[864,64]{1,0:T(8,128)(2,1)} %bitcast.22, f32[1,64]{1,0:T(1,128)} %bitcast.25, ...), custom_call_target="tpu_custom_call" | custom-call | tf_op jit(solution)/shard_map/pallas_call | solution.py:700
  80.5 0.0 copy-start.2
  80.5 1.6 %reshape.54 = bf16[128,1,4,128]{3,2,0,1:T(4,128)(2,1)} reshape(bf16[128,512]{1,0:T(8,128)(2,1)} %get-tuple-element.12) | data formatting | bytes 262144 | tf_op jit(solution)/shard_map/reshape | solution.py:712
  82.1 0.0 copy-done.2
  82.1 0.5 copy.17
  82.6 0.0 copy-start.1
  82.6 0.0 copy-start.4
  82.6 2.9 %copy.19 = bf16[32,32,8,16]{1,3,2,0:T(8,128)(2,1)} copy(bf16[32,32,8,16]{0,3,2,1:T(8,128)(2,1)S(1)} %bitcast.16) | data formatting | bytes 524288
  85.5 0.0 copy-done.1
  85.5 0.0 copy-start
  85.5 0.8 copy.27
  86.3 0.0 copy-done.4
  86.3 0.5 copy.28
  86.8 0.0 copy-done
  86.9 0.0 copy-start.3
  86.9 0.9 %copy.29 = f32[3,3,3,64,128]{4,3,2,1,0:T(8,128)} copy(f32[3,3,3,64,128]{4,3,2,1,0:T(8,128)S(1)} %bitcast.18) | data formatting | bytes 1769472
  87.8 0.0 copy-done.3
  87.8 0.5 copy.30
Async XLA Ops:
  80.5 1.6 %copy-start.2 = (bf16[32,4096]{1,0:T(8,128)(2,1)S(1)}, bf16[32,4096]{1,0:T(8,128)(2,1)}, u32[]{:S(2)}) copy-start(bf16[32,4096]{1,0:T(8,128)(2,1)} %get-tuple-element.13) | copy-start | bytes 786436
  82.6 2.9 %copy-start.1 = (f32[864,64]{1,0:T(8,128)S(1)}, f32[864,64]{1,0:T(8,128)}, u32[]{:S(2)}) copy-start(f32[864,64]{1,0:T(8,128)} %get-tuple-element.14) | copy-start | bytes 663556
  82.6 3.7 %copy-start.4 = (f32[1,64]{1,0:T(1,128)S(1)}, f32[1,64]{1,0:T(1,128)}, u32[]{:S(2)}) copy-start(f32[1,64]{1,0:T(1,128)} %get-tuple-element.15) | copy-start | bytes 772
  85.5 1.3 %copy-start = (f32[1728,128]{1,0:T(8,128)S(1)}, f32[1728,128]{1,0:T(8,128)}, u32[]{:S(2)}) copy-start(f32[1728,128]{1,0:T(8,128)} %get-tuple-element.16) | copy-start | bytes 2654212
  86.9 0.9 %copy-start.3 = (f32[1,128]{1,0:T(1,128)S(1)}, f32[1,128]{1,0:T(1,128)}, u32[]{:S(2)}) copy-start(f32[1,128]{1,0:T(1,128)} %get-tuple-element.17) | copy-start | bytes 1540

commit v3 on v2

--- a/solution.py
+++ b/solution.py
@@ -66,7 +66,7 @@
 class Exchange:
     def __init__(self, grid, channels, buffers, sems, at):
         self.grid, self.channels = grid, channels
-        self.zs, self.zr, self.ys, self.yr, self.cs, self.cr, self.xs, self.xr = buffers
+        self.zs, self.zr, self.ys, self.yr, self.cs, self.cr, self.xs, self.xr, self.ds, self.dr = buffers
         self.gx, self.gy, self.gz = [lax.axis_index(axis) for axis in ("gx", "gy", "gz")]
         cuts_y, cuts_z = lax.axis_size("gy"), lax.axis_size("gz")
         moves = []
@@ -75,7 +75,9 @@
             moves.append((self.ys.at[side], self.yr.at[side], 0, step[side], 0))
         for dy in NEAR:
             for dz in NEAR:
-                moves.append((self.xs, self.xr.at[(1 - dy) * 3 + 1 - dz], 1, dy, dz))
+                source = self.ds.at[(1 - dy) // 2] if dy else self.xs
+                target = self.dr.at[(1 - dy) // 2, 1 - dz] if dy else self.xr.at[1 - dz]
+                moves.append((source, target, 1, dy, dz))
         for side in BOTH:
             moves.append((self.zs.at[side], self.zr.at[side], 0, 0, step[side]))
         for sy in BOTH:
@@ -101,7 +103,7 @@
             self.moves.append((copy, goes, comes))
 
     def clear(self):
-        for ref in (self.zr, self.yr, self.cr, self.xr):
+        for ref in (self.zr, self.yr, self.cr, self.xr, self.dr):
             ref[...] = jnp.zeros_like(ref)
 
     def pack(self, field):
@@ -124,6 +126,19 @@
                 made.append(out)
             self.xs[...] = jnp.where(place * 0 + self.gx == 0, *made)
 
+        groups = c // 16
+        block = lax.broadcasted_iota(jnp.int32, (16, LANES), 1) // grid.nz
+        for side in BOTH:
+            made = []
+            for end, i in zip(ends, (grid.fold - 1, 0)):
+                here = i * grid.ny + (last_y if side == 0 else 0)
+                out = None
+                for j in range(groups):
+                    piece = roll(end[16 * j : 16 * j + 16], grid.nz * (j - here))
+                    out = piece if out is None else jnp.where(block == j, piece, out)
+                made.append(out)
+            self.ds[side] = jnp.where(block * 0 + self.gx == 0, *made)
+
         def one(q, carry):
             held = [None, None]
             rows = [None, None]
@@ -186,24 +201,31 @@
     def beyond(self):
         grid, c = self.grid, self.channels
         _, y, z = grid.at(c)
+        last = grid.fold - 1
         if grid.fold == 1:
-            came = [self.xr[i] for i in range(9)]
+            came = [self.xr[i] for i in range(3)]
         else:
-            last = grid.fold - 1
             came = [
                 jnp.concatenate([roll(self.xr[i], grid.plane * (last - j)) for j in range(grid.fold)], axis=0)
-                for i in range(9)
+                for i in range(3)
             ]
-        along = grid.nz * (grid.ny - 1)
+        over = []
+        for side in BOTH:
+            to = last * grid.ny + (0 if side == 0 else grid.ny - 1)
+            over.append(
+                [
+                    jnp.concatenate(
+                        [roll(self.dr[side, i], grid.nz * (to - j)) for j in range(c // 16)], axis=0
+                    )
+                    for i in range(3)
+                ]
+            )
         rows = []
-        for dy in range(3):
-            low, here, high = came[dy * 3 : dy * 3 + 3]
+        for low, here, high in (over[0], came, over[1]):
             low, high = roll(low, 1 - grid.nz), roll(high, grid.nz - 1)
             rows.append([self.shift_z(here, low, high, dz, z) for dz in NEAR])
         return [
-            self.shift_y(rows[1][dz], roll(rows[0][dz], -along), roll(rows[2][dz], along), dy, y)
-            for dy in NEAR
-            for dz in range(3)
+            self.shift_y(rows[1][dz], rows[0][dz], rows[2][dz], dy, y) for dy in NEAR for dz in range(3)
         ]
 
     def strips(self, shifted):
@@ -477,9 +499,13 @@
 
 
 def whole_kernel(setting, *refs):
-    fine_size, coarse_size, scales, names = setting
+    names, local = setting[3:]
+    pl.run_scoped(lambda **held: stages(setting, dict(zip(names, refs)) | held), **local)
+
+
+def stages(setting, named):
+    fine_size, coarse_size, scales = setting[:3]
     fine, coarse = Grid(*fine_size), Grid(*coarse_size)
-    named = dict(zip(names, refs))
     r = lambda name: named[name]
     fields = ("a", "b", "gb", "ga")
     grids = (fine, coarse, coarse, fine)
@@ -493,7 +519,7 @@
         name: Exchange(
             grid,
             widths[name],
-            [r(name + part) for part in ("_zs", "_zr", "_ys", "_yr", "_cs", "_cr", "_xs", "_xr")],
+            [r(name + part) for part in ("_zs", "_zr", "_ys", "_yr", "_cs", "_cr", "_xs", "_xr", "_ds", "_dr")],
             r("halo_sems"),
             i,
         )
@@ -510,12 +536,14 @@
     out_a, in_a, out_b, in_b, spread, thin, order = [
         r(n) for n in ("to_a", "from_a", "to_b", "from_b", "spread", "thin", "order")
     ]
+    field = r("field")
     bf16 = jnp.bfloat16
 
     for name in fields:
         halos[name].clear()
     barrier, arrivals = greet()
-    halos["a"].pack(volume)
+    field[...] = volume[...]
+    halos["a"].pack(field)
     order[...] = order_map(coarse, lax.axis_size("gz"))
     mixed[...] = dot(cot[...], order[...]).astype(bf16)
     pl.semaphore_wait(barrier, arrivals)
@@ -539,7 +567,7 @@
     acc_b[...] = jnp.zeros_like(acc_b)
 
     halos["a"].wait()
-    halos["a"].fine_windows(volume, strips["a"], win_a)
+    halos["a"].fine_windows(field, strips["a"], win_a)
     many = 2 * coarse.fold
 
     def forward_a(g, carry):
@@ -602,6 +630,7 @@
     sum_b.middle()
     halos["ga"].wait()
     halos["ga"].fine_windows(grad_a, strips["ga"], win_ga)
+    sum_a.middle()
 
     def backward_a(g, carry):
         total = dot(in_a[0], win_ga[:, lanes_at(g * many, many)])
@@ -611,10 +640,9 @@
         return carry
 
     lax.fori_loop(0, coarse.tiles, backward_a, 0)
-    sum_a.middle()
+    sum_b.last()
     feats.unpack(feat)
     features[...] = dot_rows(feat[...], order[...]).astype(bf16)
-    sum_b.last()
     sum_a.last()
     sum_b.finish()
     all_a, all_b = r("sum_a4"), r("sum_b4")
@@ -660,23 +688,26 @@
         "out_wb": ((27 * c2, c3), f32),
         "out_bb": ((1, c3), f32),
     }
-    scratch = {}
+    scratch, local = {}, {}
     for name, grid, c in (("a", fine, c1), ("b", coarse, c2), ("gb", coarse, c3), ("ga", fine, c2)):
         for end in ("s", "r"):
             scratch[f"{name}_z{end}"] = pltpu.VMEM((2, c, grid.zpacks * LANES), bf16)
             scratch[f"{name}_y{end}"] = pltpu.VMEM((2, c, grid.ypacks * LANES), bf16)
             scratch[f"{name}_c{end}"] = pltpu.VMEM((4, c // grid.corner_groups(c), LANES), bf16)
         scratch[f"{name}_xs"] = pltpu.VMEM((c // grid.fold, LANES), bf16)
-        scratch[f"{name}_xr"] = pltpu.VMEM((9, c // grid.fold, LANES), bf16)
-        scratch[f"{name}_strips"] = pltpu.VMEM((6, c, grid.ypacks * LANES), bf16)
+        scratch[f"{name}_xr"] = pltpu.VMEM((3, c // grid.fold, LANES), bf16)
+        scratch[f"{name}_ds"] = pltpu.VMEM((2, 16, LANES), bf16)
+        scratch[f"{name}_dr"] = pltpu.VMEM((2, 3, 16, LANES), bf16)
+        local[f"{name}_strips"] = pltpu.VMEM((6, c, grid.ypacks * LANES), bf16)
         shape = (9 * c, (grid.tiles + 2) * LANES) if grid is fine else (27 * c, grid.tiles * LANES)
-        scratch[f"{name}_win"] = pltpu.VMEM(shape, bf16)
-    scratch["before_a"] = pltpu.VMEM((c2, cells), f32)
-    scratch["pooled"] = pltpu.VMEM((c2, fewer), bf16)
-    scratch["grad_b"] = pltpu.VMEM((c3, fewer), bf16)
-    scratch["grad_a"] = pltpu.VMEM((c2, cells), bf16)
-    scratch["mixed"] = pltpu.VMEM((c3, fewer), bf16)
-    scratch["feat"] = pltpu.VMEM((c3, fewer), bf16)
+        local[f"{name}_win"] = pltpu.VMEM(shape, bf16)
+    local["field"] = pltpu.VMEM((c1, cells), bf16)
+    local["before_a"] = pltpu.VMEM((c2, cells), f32)
+    local["pooled"] = pltpu.VMEM((c2, fewer), bf16)
+    local["grad_b"] = pltpu.VMEM((c3, fewer), bf16)
+    local["grad_a"] = pltpu.VMEM((c2, cells), bf16)
+    local["mixed"] = pltpu.VMEM((c3, fewer), bf16)
+    local["feat"] = pltpu.VMEM((c3, fewer), bf16)
     for name, rows in (("a", rows_a), ("b", rows_b)):
         chunk = rows // members
         scratch[f"acc_{name}"] = pltpu.VMEM((rows, LANES), f32)
@@ -686,19 +717,19 @@
             scratch[f"sum_{name}{i}"] = pltpu.VMEM((*shape, LANES), bf16)
     for name in ("cot_sent", "cot_came", "feat_sent", "feat_came"):
         scratch[name] = pltpu.VMEM((levels, c3 // coarse.fold, LANES), bf16)
-    scratch["to_a"] = pltpu.VMEM((3, c2, 9 * c1), bf16)
-    scratch["from_a"] = pltpu.VMEM((3, c1, 9 * c2), bf16)
-    scratch["to_b"] = pltpu.VMEM((c3, 27 * c2), bf16)
-    scratch["from_b"] = pltpu.VMEM((c2, 27 * c3), bf16)
-    scratch["spread"] = pltpu.VMEM((LANES, coarse.fold * LANES), bf16)
-    scratch["thin"] = pltpu.VMEM((LANES, coarse.fold * LANES), bf16)
-    scratch["order"] = pltpu.VMEM((fewer, fewer), bf16)
+    local["to_a"] = pltpu.VMEM((3, c2, 9 * c1), bf16)
+    local["from_a"] = pltpu.VMEM((3, c1, 9 * c2), bf16)
+    local["to_b"] = pltpu.VMEM((c3, 27 * c2), bf16)
+    local["from_b"] = pltpu.VMEM((c2, 27 * c3), bf16)
+    local["spread"] = pltpu.VMEM((LANES, coarse.fold * LANES), bf16)
+    local["thin"] = pltpu.VMEM((LANES, coarse.fold * LANES), bf16)
+    local["order"] = pltpu.VMEM((fewer, fewer), bf16)
     scratch["halo_sems"] = pltpu.SemaphoreType.DMA((2, 4, 17))
     scratch["sum_sems"] = pltpu.SemaphoreType.DMA((2, 3, 2, max(members, levels)))
     scratch["slab_sems"] = pltpu.SemaphoreType.DMA((2, 2, levels))
     names = (*operands, *outs, *scratch)
     got = pl.pallas_call(
-        functools.partial(whole_kernel, (fine_size, coarse_size, (scale_a, scale_b), names)),
+        functools.partial(whole_kernel, (fine_size, coarse_size, (scale_a, scale_b), names, local)),
         out_shape=[jax.ShapeDtypeStruct(shape, dtype) for shape, dtype in outs.values()],
         in_specs=[pl.BlockSpec(memory_space=pltpu.VMEM)] * len(operands),
         out_specs=[pl.BlockSpec(memory_space=pltpu.VMEM)] * len(outs),

time: 88.5 us -> 84.7 us (0.957)
  Pallas kernels: 74 us -> 70.2 us
    pallas_call x1, Pallas kernels: 74 us -> 70.2 us  [on_device(): pl.pallas_call(functools.partial(whole_kernel, (fine_size, coarse_size, (...]
where the time goes in v3:
time: 84.7 us; the launch traced here: 84.5 us
  Pallas kernels  70.2 us (83%)
  local copies, waits for them, and re-layouts  13.6 us (16%)
    pallas_call x1, Pallas kernels, on_device(): pl.pallas_call(functools.partial(whole_kernel, (fine_size, coarse_size, (...  70.2 us
    unnamed x17, local copies, waits for them, and re-layouts  10.5 us

profile of v3, /device:TPU:1, one launch (start us, length us, event | category | flops | bytes accessed | tf_op | source)
XLA Modules:
  0.0 84.5 jit_solution(2927835612195226587)
XLA Ops:
  0.6 1.6 %copy.22 = bf16[16,8,4,128]{3,1,2,0:T(8,128)(2,1)} copy(bf16[16,8,4,128]{3,2,1,0:T(4,128)(2,1)} %bitcast.23) | data formatting | bytes 262144
  2.2 3.2 %copy.15 = bf16[32,32,8,16]{0,3,2,1:T(8,128)(2,1)S(1)} copy(bf16[32,32,8,16]{1,3,2,0:T(8,128)(2,1)} %param.6) | data formatting | bytes 524288 | tf_op args[0]
  5.4 1.0 %copy.16.refs_0_ = bf16[32,4096]{1,0:T(8,128)(2,1)} copy(bf16[32,4096]{0,1:T(8,128)(2,1)S(1)} %bitcast.17) | data formatting | bytes 524288 | tf_op jit(solution)/shard_map/reshape | solution.py:676
  6.5 70.2 %shard_map.109 = (bf16[128,512]{1,0:T(8,128)(2,1)}, bf16[32,4096]{1,0:T(8,128)(2,1)}, f32[864,64]{1,0:T(8,128)}, f32[1,64]{1,0:T(1,128)}, f32[1728,128]{1,0:T(8,128)}, /*index=5*/f32[1,128]{1,0:T(1,128)}) custom-call(bf16[32,4096]{1,0:T(8,128)(2,1)} %copy.16.refs_0_, bf16[864,64]{1,0:T(8,128)(2,1)} %bitcast.22, f32[1,64]{1,0:T(1,128)} %bitcast.25, ...), custom_call_target="tpu_custom_call" | custom-call | tf_op jit(solution)/shard_map/pallas_call | solution.py:731
  76.7 0.0 copy-start.2
  76.7 1.6 %reshape.54 = bf16[128,1,4,128]{3,2,0,1:T(4,128)(2,1)} reshape(bf16[128,512]{1,0:T(8,128)(2,1)} %get-tuple-element.12) | data formatting | bytes 262144 | tf_op jit(solution)/shard_map/reshape | solution.py:743
  78.3 0.0 copy-done.2
  78.3 0.5 copy.17
  78.8 0.0 copy-start.1
  78.8 0.0 copy-start.4
  78.8 2.9 %copy.19 = bf16[32,32,8,16]{1,3,2,0:T(8,128)(2,1)} copy(bf16[32,32,8,16]{0,3,2,1:T(8,128)(2,1)S(1)} %bitcast.16) | data formatting | bytes 524288
  81.8 0.0 copy-done.1
  81.8 0.0 copy-start
  81.8 0.8 copy.27
  82.5 0.0 copy-done.4
  82.5 0.5 copy.28
  83.0 0.0 copy-done
  83.1 0.0 copy-start.3
  83.1 0.9 %copy.29 = f32[3,3,3,64,128]{4,3,2,1,0:T(8,128)} copy(f32[3,3,3,64,128]{4,3,2,1,0:T(8,128)S(1)} %bitcast.18) | data formatting | bytes 1769472
  84.0 0.0 copy-done.3
  84.0 0.5 copy.30
Async XLA Ops:
  76.7 1.6 %copy-start.2 = (bf16[32,4096]{1,0:T(8,128)(2,1)S(1)}, bf16[32,4096]{1,0:T(8,128)(2,1)}, u32[]{:S(2)}) copy-start(bf16[32,4096]{1,0:T(8,128)(2,1)} %get-tuple-element.13) | copy-start | bytes 786436
  78.8 2.9 %copy-start.1 = (f32[864,64]{1,0:T(8,128)S(1)}, f32[864,64]{1,0:T(8,128)}, u32[]{:S(2)}) copy-start(f32[864,64]{1,0:T(8,128)} %get-tuple-element.14) | copy-start | bytes 663556
  78.8 3.7 %copy-start.4 = (f32[1,64]{1,0:T(1,128)S(1)}, f32[1,64]{1,0:T(1,128)}, u32[]{:S(2)}) copy-start(f32[1,64]{1,0:T(1,128)} %get-tuple-element.15) | copy-start | bytes 772
  81.8 1.3 %copy-start = (f32[1728,128]{1,0:T(8,128)S(1)}, f32[1728,128]{1,0:T(8,128)}, u32[]{:S(2)}) copy-start(f32[1728,128]{1,0:T(8,128)} %get-tuple-element.16) | copy-start | bytes 2654212
  83.1 0.9 %copy-start.3 = (f32[1,128]{1,0:T(1,128)S(1)}, f32[1,128]{1,0:T(1,128)}, u32[]{:S(2)}) copy-start(f32[1,128]{1,0:T(1,128)} %get-tuple-element.17) | copy-start | bytes 1540

commit v4 on v3

--- a/solution.py
+++ b/solution.py
@@ -10,6 +10,7 @@
 
 MESH = pl.DeviceIdType.MESH
 LANES = 128
+PITCH = 40
 BOTH = (0, 1)
 NEAR = (-1, 0, 1)
 
@@ -305,9 +306,9 @@
 
 
 class Summing:
-    def __init__(self, acc, stage, first, mine, second, whole, sems):
+    def __init__(self, acc, stage, first, mine, second, whole, third, sems):
         self.acc, self.stage, self.first = acc, stage, first
-        self.mine, self.second, self.whole = mine, second, whole
+        self.mine, self.second, self.whole, self.third = mine, second, whole, third
         self.sems = sems
         gy = lax.axis_size("gy")
         self.count = lax.axis_size("gx") * gy
@@ -315,40 +316,44 @@
         self.me = lax.axis_index("gx") * gy + lax.axis_index("gy")
         self.level = lax.axis_index("gz")
 
-    def across(self, phase, k, source, target):
-        gy = lax.axis_size("gy")
-        to = (self.me + k) % self.count
+    def copy(self, phase, k, source, target, device):
         return pltpu.make_async_remote_copy(
-            src_ref=source(to),
+            src_ref=source,
             dst_ref=target,
             send_sem=self.sems.at[phase, 0, k],
             recv_sem=self.sems.at[phase, 1, k],
-            device_id={"gx": to // gy, "gy": to % gy},
+            device_id=device,
             device_id_type=MESH,
         )
 
-    def along(self, k):
-        return pltpu.make_async_remote_copy(
-            src_ref=self.mine,
-            dst_ref=self.second.at[self.level],
-            send_sem=self.sems.at[1, 0, k],
-            recv_sem=self.sems.at[1, 1, k],
-            device_id={"gz": (self.level + k) % self.depth},
-            device_id_type=MESH,
-        )
+    def across(self, phase, source, target):
+        gy, out = lax.axis_size("gy"), []
+        for k in range(1, self.count):
+            to = (self.me + k) % self.count
+            out.append(self.copy(phase, k, source(to), target, {"gx": to // gy, "gy": to % gy}))
+        return out
+
+    def along(self, phase, source, target):
+        out = []
+        for k in range(1, self.depth):
+            to = (self.level + k) % self.depth
+            out.append(self.copy(phase, k, source(to), target, {"gz": to}))
+        return out
 
     def scatters(self):
-        return [
-            self.across(0, k, lambda to: self.stage.at[to], self.first.at[self.me])
-            for k in range(1, self.count)
-        ]
+        return self.across(0, lambda to: self.stage.at[to], self.first.at[self.me])
 
     def alongs(self):
-        return [self.along(k) for k in range(1, self.depth)]
+        source = (lambda to: self.mine) if self.third is None else (lambda to: self.mine.at[to])
+        return self.along(1, source, self.second.at[self.level])
+
+    def returns(self):
+        here = self.third.at[self.level]
+        return self.along(3, lambda to: here, here)
 
     def gathers(self):
         here = self.whole.at[self.me]
-        return [self.across(2, k, lambda to: here, here) for k in range(1, self.count)]
+        return self.across(2, lambda to: here, here)
 
     def start(self):
         chunk = self.stage.shape[1]
@@ -362,21 +367,33 @@
         total = parts[0].astype(jnp.float32)
         for i in range(1, parts.shape[0]):
             total = total + parts[i].astype(jnp.float32)
-        return total.astype(jnp.bfloat16)
+        return total
 
     def middle(self):
         for copy in self.scatters():
             copy.wait()
-        part = self.total(self.first)
-        self.mine[...] = part
+        self.mine[...] = self.total(self.first).reshape(self.mine.shape).astype(jnp.bfloat16)
         for copy in self.alongs():
             copy.start()
-        self.second[self.level] = part
-
-    def last(self):
+        self.second[self.level] = self.mine[...] if self.third is None else self.mine[self.level]
+
+    def between(self):
         for copy in self.alongs():
             copy.wait()
-        self.whole[self.me] = self.total(self.second)
+        self.third[self.level] = self.total(self.second).astype(jnp.bfloat16)
+        for copy in self.returns():
+            copy.start()
+
+    def last(self):
+        if self.third is None:
+            for copy in self.alongs():
+                copy.wait()
+            total = self.total(self.second)
+        else:
+            for copy in self.returns():
+                copy.wait()
+            total = self.third[...].astype(jnp.float32).reshape(self.whole.shape[1:])
+        self.whole[self.me] = total.astype(jnp.bfloat16)
         for copy in self.gathers():
             copy.start()
 
@@ -498,6 +515,30 @@
     return jnp.sum(jnp.where(across == down, row, 0.0), axis=1, keepdims=True)
 
 
+def turn_in(volume, rows, field):
+    channels, _, nx = volume.shape
+    fold = LANES // nx
+    for q in range(channels // fold):
+        wide = jnp.concatenate([volume[q * fold + i] for i in range(fold)], axis=1)
+        turned = wide.astype(jnp.float32).T
+        for i in range(fold):
+            begin = (q * fold + i) * PITCH
+            rows[begin : begin + nx] = turned[i * nx : (i + 1) * nx]
+    for x in range(nx):
+        field[:, lanes_at(x)] = rows[pl.ds(x, channels, stride=PITCH), :].astype(jnp.bfloat16)
+
+
+def turn_out(rows, out):
+    channels, _, nx = out.shape
+    fold = LANES // nx
+    for q in range(channels // fold):
+        begins = [(q * fold + i) * PITCH for i in range(fold)]
+        wide = jnp.concatenate([rows[begin : begin + nx] for begin in begins], axis=0)
+        turned = wide.T.astype(jnp.bfloat16)
+        for i in range(fold):
+            out[q * fold + i] = turned[:, i * nx : (i + 1) * nx]
+
+
 def whole_kernel(setting, *refs):
     names, local = setting[3:]
     pl.run_scoped(lambda **held: stages(setting, dict(zip(names, refs)) | held), **local)
@@ -507,13 +548,14 @@
     fine_size, coarse_size, scales = setting[:3]
     fine, coarse = Grid(*fine_size), Grid(*coarse_size)
     r = lambda name: named[name]
+    field = r("field")
     fields = ("a", "b", "gb", "ga")
     grids = (fine, coarse, coarse, fine)
     volume, w_a, b_a, w_b, b_b, cot = [r(n) for n in ("volume", "w_a", "b_a", "w_b", "b_b", "cot")]
     features, grad_in, out_wa, out_ba, out_wb, out_bb = [
         r(n) for n in ("features", "grad_in", "out_wa", "out_ba", "out_wb", "out_bb")
     ]
-    c1, c2, c3 = volume.shape[0], w_a.shape[1], w_b.shape[1]
+    c1, c2, c3 = field.shape[0], w_a.shape[1], w_b.shape[1]
     widths = dict(zip(fields, (c1, c2, c3, c2)))
     halos = {
         name: Exchange(
@@ -529,25 +571,32 @@
     win_a, win_b, win_gb, win_ga = [r(name + "_win") for name in fields]
     before_a, pooled, grad_b, grad_a = [r(n) for n in ("before_a", "pooled", "grad_b", "grad_a")]
     acc_a, acc_b, mixed, feat = [r(n) for n in ("acc_a", "acc_b", "mixed", "feat")]
-    sum_a = Summing(acc_a, *[r(f"sum_a{i}") for i in range(5)], r("sum_sems").at[0])
-    sum_b = Summing(acc_b, *[r(f"sum_b{i}") for i in range(5)], r("sum_sems").at[1])
+    sum_a = Summing(acc_a, *[r(f"sum_a{i}") for i in range(5)], None, r("sum_sems").at[0])
+    sum_b = Summing(acc_b, *[r(f"sum_b{i}") for i in range(6)], r("sum_sems").at[1])
     cots = Slabs(r("cot_sent"), r("cot_came"), r("slab_sems").at[0], coarse)
     feats = Slabs(r("feat_sent"), r("feat_came"), r("slab_sems").at[1], coarse)
     out_a, in_a, out_b, in_b, spread, thin, order = [
         r(n) for n in ("to_a", "from_a", "to_b", "from_b", "spread", "thin", "order")
     ]
-    field = r("field")
     bf16 = jnp.bfloat16
 
     for name in fields:
         halos[name].clear()
     barrier, arrivals = greet()
-    field[...] = volume[...]
+    rows_in, rows_out = r("rows_in"), r("rows_out")
+    turn_in(volume, rows_in, field)
     halos["a"].pack(field)
-    order[...] = order_map(coarse, lax.axis_size("gz"))
-    mixed[...] = dot(cot[...], order[...]).astype(bf16)
     pl.semaphore_wait(barrier, arrivals)
     halos["a"].start()
+    order[...] = order_map(coarse, lax.axis_size("gz"))
+    rows_cot = r("rows_cot")
+    rows_cot[...] = cot[...].astype(jnp.float32).reshape(rows_cot.shape)
+    total = None
+    for y in range(coarse.ny):
+        row = rows_cot[pl.ds(y, c3, stride=coarse.ny), :].astype(bf16)
+        part = dot(row, order[y * LANES : (y + 1) * LANES])
+        total = part if total is None else total + part
+    mixed[...] = total.astype(bf16)
     cots.pack(mixed)
 
     taps = 9
@@ -619,6 +668,7 @@
     lax.fori_loop(0, coarse.tiles, backward_b, 0)
     halos["ga"].pack(grad_a)
     halos["ga"].start()
+    sum_b.middle()
     grad = grad_a[...]
     half, width = out_wa.shape[0] // 2, out_wa.shape[1]
     parts = [dot_rows(win_a[:, lanes_at(dx, fine.tiles)], grad) for dx in range(3)]
@@ -627,23 +677,28 @@
     acc_a[:half, width:] = whole[half:]
     acc_a[half : half + 8, :width] = dot_rows(jnp.ones((8, grad.shape[1]), bf16), grad)
     sum_a.start()
-    sum_b.middle()
+    sum_b.between()
     halos["ga"].wait()
+    sum_a.middle()
     halos["ga"].fine_windows(grad_a, strips["ga"], win_ga)
-    sum_a.middle()
+    sum_b.last()
 
     def backward_a(g, carry):
         total = dot(in_a[0], win_ga[:, lanes_at(g * many, many)])
         for dx in (1, 2):
             total = total + dot(in_a[dx], win_ga[:, lanes_at(g * many + dx, many)])
-        grad_in[:, lanes_at(g * many, many)] = total.astype(bf16)
+        for i in range(many):
+            tile = total[:, i * LANES : (i + 1) * LANES].astype(bf16).astype(jnp.float32)
+            rows_out[pl.ds(g * many + i, c1, stride=PITCH), :] = tile
         return carry
 
     lax.fori_loop(0, coarse.tiles, backward_a, 0)
-    sum_b.last()
+    sum_a.last()
     feats.unpack(feat)
-    features[...] = dot_rows(feat[...], order[...]).astype(bf16)
-    sum_a.last()
+    for y in range(coarse.ny):
+        rows_cot[pl.ds(y, c3, stride=coarse.ny), :] = dot_rows(feat[...], order[y * LANES : (y + 1) * LANES])
+    features[...] = rows_cot[...].reshape(features.shape).astype(bf16)
+    turn_out(rows_out, grad_in)
     sum_b.finish()
     all_a, all_b = r("sum_a4"), r("sum_b4")
     scale_a, scale_b = scales
@@ -671,18 +726,18 @@
     rows_a = 27 * c1 // 2 + 16
     rows_a += -rows_a % (16 * members)
     rows_b = 27 * c2 + 16
-    rows_b += -rows_b % (16 * members)
+    rows_b += -rows_b % (8 * members * levels)
     operands = {
-        "volume": volume.reshape(c1, cells),
+        "volume": jnp.transpose(volume, (0, 2, 3, 1)).reshape(c1, ny * nz, nx),
         "w_a": weight_a.reshape(27 * c1, c2),
         "b_a": bias_a.reshape(1, c2),
         "w_b": weight_b.reshape(27 * c2, c3),
         "b_b": bias_b.reshape(1, c3),
-        "cot": cotangent.reshape(c3, fewer),
+        "cot": cotangent.reshape(c3, ny // 2, nz // 2 * levels),
     }
     outs = {
-        "features": ((c3, fewer), bf16),
-        "grad_in": ((c1, cells), bf16),
+        "features": ((c3, ny // 2, nz // 2 * levels), bf16),
+        "grad_in": ((c1, ny * nz, nx), bf16),
         "out_wa": ((27 * c1, c2), f32),
         "out_ba": ((1, c2), f32),
         "out_wb": ((27 * c2, c3), f32),
@@ -702,6 +757,8 @@
         shape = (9 * c, (grid.tiles + 2) * LANES) if grid is fine else (27 * c, grid.tiles * LANES)
         local[f"{name}_win"] = pltpu.VMEM(shape, bf16)
     local["field"] = pltpu.VMEM((c1, cells), bf16)
+    local["rows_in"] = local["rows_out"] = pltpu.VMEM((c1 * PITCH, ny * nz), f32)
+    local["rows_cot"] = pltpu.VMEM((c3 * ny // 2, nz // 2 * levels), f32)
     local["before_a"] = pltpu.VMEM((c2, cells), f32)
     local["pooled"] = pltpu.VMEM((c2, fewer), bf16)
     local["grad_b"] = pltpu.VMEM((c3, fewer), bf16)
@@ -711,9 +768,11 @@
     for name, rows in (("a", rows_a), ("b", rows_b)):
         chunk = rows // members
         scratch[f"acc_{name}"] = pltpu.VMEM((rows, LANES), f32)
-        for i, shape in enumerate(
-            ((members, chunk), (members, chunk), (chunk,), (levels, chunk), (members, chunk))
-        ):
+        shapes = [(members, chunk), (members, chunk), (chunk,), (levels, chunk), (members, chunk)]
+        if name == "b":
+            shapes[2:4] = [(levels, chunk // levels)] * 2
+            shapes.append((levels, chunk // levels))
+        for i, shape in enumerate(shapes):
             scratch[f"sum_{name}{i}"] = pltpu.VMEM((*shape, LANES), bf16)
     for name in ("cot_sent", "cot_came", "feat_sent", "feat_came"):
         scratch[name] = pltpu.VMEM((levels, c3 // coarse.fold, LANES), bf16)
@@ -725,7 +784,7 @@
     local["thin"] = pltpu.VMEM((LANES, coarse.fold * LANES), bf16)
     local["order"] = pltpu.VMEM((fewer, fewer), bf16)
     scratch["halo_sems"] = pltpu.SemaphoreType.DMA((2, 4, 17))
-    scratch["sum_sems"] = pltpu.SemaphoreType.DMA((2, 3, 2, max(members, levels)))
+    scratch["sum_sems"] = pltpu.SemaphoreType.DMA((2, 4, 2, max(members, levels)))
     scratch["slab_sems"] = pltpu.SemaphoreType.DMA((2, 2, levels))
     names = (*operands, *outs, *scratch)
     got = pl.pallas_call(
@@ -741,7 +800,7 @@
     features, grad_in, sum_wa, sum_ba, sum_wb, sum_bb = got
     return (
         features.reshape(cotangent.shape),
-        grad_in.reshape(volume.shape),
+        jnp.transpose(grad_in.reshape(c1, ny, nz, nx), (0, 3, 1, 2)),
         sum_wa.reshape(weight_a.shape),
         sum_ba.reshape(c2),
         sum_wb.reshape(weight_b.shape),

time: 84.7 us -> 75.2 us (0.89)
  local copies, waits for them, and re-layouts: 13.6 us -> 6.9 us
  Pallas kernels: 70.2 us -> 67.4 us
    unnamed x17 -> x14, local copies, waits for them, and re-layouts: 10.5 us -> 6.9 us
    pallas_call x1, Pallas kernels: 70.2 us -> 67.4 us  [on_device(): pl.pallas_call(functools.partial(whole_kernel, (fine_size, coarse_size, (...]
    reshape x2 -> x0, local copies, waits for them, and re-layouts: 2.66 us -> none  [the longest x1 1.64 us: on_device(): features.reshape(cotangent.shape)]
where the time goes in v4:
time: 75.2 us; the launch traced here: 75 us
  Pallas kernels  67.4 us (90%)
  local copies, waits for them, and re-layouts  6.9 us (9%)
    pallas_call x1, Pallas kernels, on_device(): pl.pallas_call(functools.partial(whole_kernel, (fine_size, coarse_size, (...  67.4 us
    unnamed x14, local copies, waits for them, and re-layouts  6.9 us

profile of v4, /device:TPU:1, one launch (start us, length us, event | category | flops | bytes accessed | tf_op | source)
XLA Modules:
  0.0 75.0 jit_solution(4315144784764284664)
XLA Ops:
  0.6 67.4 %shard_map.109 = (bf16[128,4,128]{2,1,0:T(4,128)(2,1)}, bf16[32,128,32]{2,1,0:T(8,128)(2,1)}, f32[864,64]{1,0:T(8,128)}, f32[1,64]{1,0:T(1,128)}, f32[1728,128]{1,0:T(8,128)}, /*index=5*/f32[1,128]{1,0:T(1,128)}) custom-call(bf16[32,128,32]{2,1,0:T(8,128)(2,1)} %bitcast.18, bf16[864,64]{1,0:T(8,128)(2,1)} %bitcast.23, f32[1,64]{1,0:T(1,128)} %bitcast.26, ...), custom_call_target="tpu_custom_call" | custom-call | tf_op jit(solution)/shard_map/pallas_call | solution.py:790
  68.1 1.6 %copy.19 = bf16[128,1,4,128]{3,2,1,0:T(4,128)(2,1)} copy(bf16[128,1,4,128]{3,2,1,0:T(4,128)(2,1)} %bitcast.25) | data formatting | bytes 262144
  69.7 0.0 copy-start.1
  69.7 0.0 copy-start.3
  69.7 2.5 %copy.20 = bf16[32,32,8,16]{1,3,2,0:T(8,128)(2,1)} copy(bf16[32,32,8,16]{1,3,2,0:T(8,128)(2,1)} %bitcast.19) | data formatting | bytes 524288
  72.2 0.0 copy-done.1
  72.2 0.0 copy-start
  72.2 0.8 %copy.21 = f32[3,3,3,32,64]{4,3,2,1,0:T(8,128)} copy(f32[3,3,3,32,64]{4,3,2,1,0:T(8,128)S(1)} %bitcast.22) | data formatting | bytes 442368
  73.0 0.0 copy-done.3
  73.0 0.5 copy.22
  73.5 0.0 copy-done
  73.6 0.0 copy-start.2
  73.6 0.9 %copy.23 = f32[3,3,3,64,128]{4,3,2,1,0:T(8,128)} copy(f32[3,3,3,64,128]{4,3,2,1,0:T(8,128)S(1)} %bitcast.20) | data formatting | bytes 1769472
  74.5 0.0 copy-done.2
  74.5 0.5 copy.24
Async XLA Ops:
  69.7 2.5 %copy-start.1 = (f32[864,64]{1,0:T(8,128)S(1)}, f32[864,64]{1,0:T(8,128)}, u32[]{:S(2)}) copy-start(f32[864,64]{1,0:T(8,128)} %get-tuple-element.14) | copy-start | bytes 663556
  69.7 3.3 %copy-start.3 = (f32[1,64]{1,0:T(1,128)S(1)}, f32[1,64]{1,0:T(1,128)}, u32[]{:S(2)}) copy-start(f32[1,64]{1,0:T(1,128)} %get-tuple-element.15) | copy-start | bytes 772
  72.2 1.3 %copy-start = (f32[1728,128]{1,0:T(8,128)S(1)}, f32[1728,128]{1,0:T(8,128)}, u32[]{:S(2)}) copy-start(f32[1728,128]{1,0:T(8,128)} %get-tuple-element.16) | copy-start | bytes 2654212
  73.6 0.9 %copy-start.2 = (f32[1,128]{1,0:T(1,128)S(1)}, f32[1,128]{1,0:T(1,128)}, u32[]{:S(2)}) copy-start(f32[1,128]{1,0:T(1,128)} %get-tuple-element.17) | copy-start | bytes 1540

commit v5 on v4

--- a/solution.py
+++ b/solution.py
@@ -85,7 +85,7 @@
             for sz in BOTH:
                 i = sy * 2 + sz
                 moves.append((self.cs.at[i], self.cr.at[i], 0, step[sy], step[sz]))
-        self.moves = []
+        self.moves, self.targets = [], []
         for i, (source, target, across, dy, dz) in enumerate(moves):
             copy = pltpu.make_async_remote_copy(
                 src_ref=source,
@@ -102,10 +102,15 @@
             goes = within(self.gy + dy, cuts_y) & within(self.gz + dz, cuts_z)
             comes = within(self.gy - dy, cuts_y) & within(self.gz - dz, cuts_z)
             self.moves.append((copy, goes, comes))
+            if dy or dz:
+                self.targets.append((target, comes))
 
     def clear(self):
-        for ref in (self.zr, self.yr, self.cr, self.xr, self.dr):
-            ref[...] = jnp.zeros_like(ref)
+        for target, comes in self.targets:
+
+            @pl.when(jnp.logical_not(comes))
+            def _(target=target):
+                target[...] = jnp.zeros(target.shape, jnp.bfloat16)
 
     def pack(self, field):
         grid, c = self.grid, self.channels
@@ -305,6 +310,22 @@
                 windows[rows[2], lanes_at(t)] = jnp.where(spot == grid.fold - 1, after, down[t])
 
 
+def ring(step, count):
+    return min(step, count - step)
+
+
+def far_first(count, hops):
+    return sorted(range(1, count), key=hops, reverse=True)
+
+
+def across_at(k):
+    gx, gy = lax.axis_size("gx"), lax.axis_size("gy")
+    high, low = gy // 4, 4
+    row = lax.axis_index("gy")
+    x = (row // low * gx + lax.axis_index("gx") + k // low) % (gx * high)
+    return x % gx, x // gx * low + (row + k) % low
+
+
 class Summing:
     def __init__(self, acc, stage, first, mine, second, whole, third, sems):
         self.acc, self.stage, self.first = acc, stage, first
@@ -328,14 +349,15 @@
 
     def across(self, phase, source, target):
         gy, out = lax.axis_size("gy"), []
-        for k in range(1, self.count):
-            to = (self.me + k) % self.count
-            out.append(self.copy(phase, k, source(to), target, {"gx": to // gy, "gy": to % gy}))
+        for k in far_first(self.count, lambda k: ring(k // 4, self.count // 4) + ring(k % 4, 4)):
+            gx, row = across_at(k)
+            to = gx * gy + row
+            out.append(self.copy(phase, k, source(to), target, {"gx": gx, "gy": row}))
         return out
 
     def along(self, phase, source, target):
         out = []
-        for k in range(1, self.depth):
+        for k in far_first(self.depth, lambda k: ring(k, self.depth)):
             to = (self.level + k) % self.depth
             out.append(self.copy(phase, k, source(to), target, {"gz": to}))
         return out
@@ -409,7 +431,7 @@
 
     def copies(self):
         out = []
-        for k in range(1, self.depth):
+        for k in far_first(self.depth, lambda k: ring(k, self.depth)):
             to = (self.level + k) % self.depth
             out.append(
                 pltpu.make_async_remote_copy(
@@ -580,16 +602,23 @@
     ]
     bf16 = jnp.bfloat16
 
-    for name in fields:
-        halos[name].clear()
+    loads = {
+        name: pltpu.make_async_copy(r(name + "_hbm"), r(name), r("load_sems").at[i])
+        for i, name in enumerate(("volume", "cot", "w_a", "w_b"))
+    }
+    for load in loads.values():
+        load.start()
     barrier, arrivals = greet()
+    halos["a"].clear()
     rows_in, rows_out = r("rows_in"), r("rows_out")
+    loads["volume"].wait()
     turn_in(volume, rows_in, field)
     halos["a"].pack(field)
     pl.semaphore_wait(barrier, arrivals)
     halos["a"].start()
     order[...] = order_map(coarse, lax.axis_size("gz"))
     rows_cot = r("rows_cot")
+    loads["cot"].wait()
     rows_cot[...] = cot[...].astype(jnp.float32).reshape(rows_cot.shape)
     total = None
     for y in range(coarse.ny):
@@ -599,6 +628,8 @@
     mixed[...] = total.astype(bf16)
     cots.pack(mixed)
 
+    loads["w_a"].wait()
+    loads["w_b"].wait()
     taps = 9
     for dx in range(3):
         out_a[dx] = w_a[dx * taps * c1 : (dx + 1) * taps * c1].T
@@ -611,6 +642,8 @@
     wide, narrow = spread_map(fine, coarse)
     spread[...] = wide
     thin[...] = narrow
+    for name in fields[1:]:
+        halos[name].clear()
     bias_a, bias_b = column_of(b_a[...]), column_of(b_b[...])
     acc_a[...] = jnp.zeros_like(acc_a)
     acc_b[...] = jnp.zeros_like(acc_b)
@@ -679,9 +712,9 @@
     sum_a.start()
     sum_b.between()
     halos["ga"].wait()
+    sum_b.last()
     sum_a.middle()
     halos["ga"].fine_windows(grad_a, strips["ga"], win_ga)
-    sum_b.last()
 
     def backward_a(g, carry):
         total = dot(in_a[0], win_ga[:, lanes_at(g * many, many)])
@@ -728,12 +761,12 @@
     rows_b = 27 * c2 + 16
     rows_b += -rows_b % (8 * members * levels)
     operands = {
-        "volume": jnp.transpose(volume, (0, 2, 3, 1)).reshape(c1, ny * nz, nx),
-        "w_a": weight_a.reshape(27 * c1, c2),
+        "volume_hbm": jnp.transpose(volume, (0, 2, 3, 1)).reshape(c1, ny * nz, nx),
+        "w_a_hbm": weight_a.reshape(27 * c1, c2),
         "b_a": bias_a.reshape(1, c2),
-        "w_b": weight_b.reshape(27 * c2, c3),
+        "w_b_hbm": weight_b.reshape(27 * c2, c3),
         "b_b": bias_b.reshape(1, c3),
-        "cot": cotangent.reshape(c3, ny // 2, nz // 2 * levels),
+        "cot_hbm": cotangent.reshape(c3, ny // 2, nz // 2 * levels),
     }
     outs = {
         "features": ((c3, ny // 2, nz // 2 * levels), bf16),
@@ -783,6 +816,9 @@
     local["spread"] = pltpu.VMEM((LANES, coarse.fold * LANES), bf16)
     local["thin"] = pltpu.VMEM((LANES, coarse.fold * LANES), bf16)
     local["order"] = pltpu.VMEM((fewer, fewer), bf16)
+    for name in ("volume", "cot", "w_a", "w_b"):
+        local[name] = pltpu.VMEM(operands[name + "_hbm"].shape, bf16)
+    scratch["load_sems"] = pltpu.SemaphoreType.DMA((4,))
     scratch["halo_sems"] = pltpu.SemaphoreType.DMA((2, 4, 17))
     scratch["sum_sems"] = pltpu.SemaphoreType.DMA((2, 4, 2, max(members, levels)))
     scratch["slab_sems"] = pltpu.SemaphoreType.DMA((2, 2, levels))
@@ -790,7 +826,9 @@
     got = pl.pallas_call(
         functools.partial(whole_kernel, (fine_size, coarse_size, (scale_a, scale_b), names, local)),
         out_shape=[jax.ShapeDtypeStruct(shape, dtype) for shape, dtype in outs.values()],
-        in_specs=[pl.BlockSpec(memory_space=pltpu.VMEM)] * len(operands),
+        in_specs=[
+            pl.BlockSpec(memory_space=pl.ANY if name.endswith("_hbm") else pltpu.VMEM) for name in operands
+        ],
         out_specs=[pl.BlockSpec(memory_space=pltpu.VMEM)] * len(outs),
         scratch_shapes=list(scratch.values()),
         compiler_params=pltpu.CompilerParams(

time: 75.2 us -> 73.9 us (0.983)
  Pallas kernels: 67.4 us -> 66.2 us
    pallas_call x1, Pallas kernels: 67.4 us -> 66.2 us  [on_device(): pl.pallas_call(functools.partial(whole_kernel, (fine_size, coarse_size, (...]
where the time goes in v5:
time: 73.9 us; the launch traced here: 73.7 us
  Pallas kernels  66.2 us (90%)
  local copies, waits for them, and re-layouts  6.9 us (9%)
    pallas_call x1, Pallas kernels, on_device(): pl.pallas_call(functools.partial(whole_kernel, (fine_size, coarse_size, (...  66.2 us
    unnamed x14, local copies, waits for them, and re-layouts  6.9 us

profile of v5, /device:TPU:1, one launch (start us, length us, event | category | flops | bytes accessed | tf_op | source)
XLA Modules:
  0.0 73.7 jit_solution(6424055163535024642)
XLA Ops:
  0.6 66.2 %shard_map.109 = (bf16[128,4,128]{2,1,0:T(4,128)(2,1)}, bf16[32,128,32]{2,1,0:T(8,128)(2,1)}, f32[864,64]{1,0:T(8,128)}, f32[1,64]{1,0:T(1,128)}, f32[1728,128]{1,0:T(8,128)}, /*index=5*/f32[1,128]{1,0:T(1,128)}) custom-call(bf16[32,128,32]{2,1,0:T(8,128)(2,1)} %bitcast.18, bf16[864,64]{1,0:T(8,128)(2,1)} %bitcast.23, f32[1,64]{1,0:T(1,128)} %bitcast.26, ...), custom_call_target="tpu_custom_call" | custom-call | tf_op jit(solution)/shard_map/pallas_call | solution.py:826
  66.8 1.6 %copy.19 = bf16[128,1,4,128]{3,2,1,0:T(4,128)(2,1)} copy(bf16[128,1,4,128]{3,2,1,0:T(4,128)(2,1)} %bitcast.25) | data formatting | bytes 262144
  68.4 0.0 copy-start.1
  68.4 0.0 copy-start.3
  68.4 2.5 %copy.20 = bf16[32,32,8,16]{1,3,2,0:T(8,128)(2,1)} copy(bf16[32,32,8,16]{1,3,2,0:T(8,128)(2,1)} %bitcast.19) | data formatting | bytes 524288
  71.0 0.0 copy-done.1
  71.0 0.0 copy-start
  71.0 0.8 %copy.21 = f32[3,3,3,32,64]{4,3,2,1,0:T(8,128)} copy(f32[3,3,3,32,64]{4,3,2,1,0:T(8,128)S(1)} %bitcast.22) | data formatting | bytes 442368
  71.7 0.0 copy-done.3
  71.7 0.5 copy.22
  72.2 0.0 copy-done
  72.3 0.0 copy-start.2
  72.3 0.9 %copy.23 = f32[3,3,3,64,128]{4,3,2,1,0:T(8,128)} copy(f32[3,3,3,64,128]{4,3,2,1,0:T(8,128)S(1)} %bitcast.20) | data formatting | bytes 1769472
  73.2 0.0 copy-done.2
  73.2 0.5 copy.24
Async XLA Ops:
  68.4 2.5 %copy-start.1 = (f32[864,64]{1,0:T(8,128)S(1)}, f32[864,64]{1,0:T(8,128)}, u32[]{:S(2)}) copy-start(f32[864,64]{1,0:T(8,128)} %get-tuple-element.14) | copy-start | bytes 663556
  68.4 3.3 %copy-start.3 = (f32[1,64]{1,0:T(1,128)S(1)}, f32[1,64]{1,0:T(1,128)}, u32[]{:S(2)}) copy-start(f32[1,64]{1,0:T(1,128)} %get-tuple-element.15) | copy-start | bytes 772
  71.0 1.3 %copy-start = (f32[1728,128]{1,0:T(8,128)S(1)}, f32[1728,128]{1,0:T(8,128)}, u32[]{:S(2)}) copy-start(f32[1728,128]{1,0:T(8,128)} %get-tuple-element.16) | copy-start | bytes 2654212
  72.3 0.9 %copy-start.2 = (f32[1,128]{1,0:T(1,128)S(1)}, f32[1,128]{1,0:T(1,128)}, u32[]{:S(2)}) copy-start(f32[1,128]{1,0:T(1,128)} %get-tuple-element.17) | copy-start | bytes 1540

commit v6 on v5

--- a/solution.py
+++ b/solution.py
@@ -606,6 +606,10 @@
         name: pltpu.make_async_copy(r(name + "_hbm"), r(name), r("load_sems").at[i])
         for i, name in enumerate(("volume", "cot", "w_a", "w_b"))
     }
+    stores = {
+        name: pltpu.make_async_copy(r(name), r(name + "_out"), r("load_sems").at[4 + i])
+        for i, name in enumerate(("features", "grad_in"))
+    }
     for load in loads.values():
         load.start()
     barrier, arrivals = greet()
@@ -731,7 +735,9 @@
     for y in range(coarse.ny):
         rows_cot[pl.ds(y, c3, stride=coarse.ny), :] = dot_rows(feat[...], order[y * LANES : (y + 1) * LANES])
     features[...] = rows_cot[...].reshape(features.shape).astype(bf16)
+    stores["features"].start()
     turn_out(rows_out, grad_in)
+    stores["grad_in"].start()
     sum_b.finish()
     all_a, all_b = r("sum_a4"), r("sum_b4")
     scale_a, scale_b = scales
@@ -743,6 +749,34 @@
     out_wa[:half] = flat_a[:half, :width]
     out_wa[half:] = flat_a[:half, width:]
     out_ba[...] = flat_a[half : half + 1, :width]
+    for store in stores.values():
+        store.wait()
+
+
+def landing_kernel(count, *refs):
+    arrived, leaving, held = [refs[i * count : (i + 1) * count] for i in range(3)]
+    sems = refs[3 * count]
+    into = [pltpu.make_async_copy(arrived[i], held[i], sems.at[0, i]) for i in range(count)]
+    out = [pltpu.make_async_copy(held[i], leaving[i], sems.at[1, i]) for i in range(count)]
+    for copy in into:
+        copy.start()
+    for first, second in zip(into, out):
+        first.wait()
+        second.start()
+    for copy in out:
+        copy.wait()
+
+
+def landed(arrays):
+    count = len(arrays)
+    return pl.pallas_call(
+        functools.partial(landing_kernel, count),
+        out_shape=[jax.ShapeDtypeStruct(array.shape, array.dtype) for array in arrays],
+        in_specs=[pl.BlockSpec(memory_space=pl.ANY)] * count,
+        out_specs=[pl.BlockSpec(memory_space=pl.ANY)] * count,
+        scratch_shapes=[pltpu.VMEM(array.shape, array.dtype) for array in arrays]
+        + [pltpu.SemaphoreType.DMA((2, count))],
+    )(*arrays)
 
 
 def on_device(volume, weight_a, bias_a, weight_b, bias_b, cotangent):
@@ -769,8 +803,8 @@
         "cot_hbm": cotangent.reshape(c3, ny // 2, nz // 2 * levels),
     }
     outs = {
-        "features": ((c3, ny // 2, nz // 2 * levels), bf16),
-        "grad_in": ((c1, ny * nz, nx), bf16),
+        "features_out": ((c3, ny // 2, nz // 2 * levels), bf16),
+        "grad_in_out": ((c1, ny * nz, nx), bf16),
         "out_wa": ((27 * c1, c2), f32),
         "out_ba": ((1, c2), f32),
         "out_wb": ((27 * c2, c3), f32),
@@ -818,7 +852,9 @@
     local["order"] = pltpu.VMEM((fewer, fewer), bf16)
     for name in ("volume", "cot", "w_a", "w_b"):
         local[name] = pltpu.VMEM(operands[name + "_hbm"].shape, bf16)
-    scratch["load_sems"] = pltpu.SemaphoreType.DMA((4,))
+    for name in ("features", "grad_in"):
+        local[name] = pltpu.VMEM(*outs[name + "_out"])
+    scratch["load_sems"] = pltpu.SemaphoreType.DMA((6,))
     scratch["halo_sems"] = pltpu.SemaphoreType.DMA((2, 4, 17))
     scratch["sum_sems"] = pltpu.SemaphoreType.DMA((2, 4, 2, max(members, levels)))
     scratch["slab_sems"] = pltpu.SemaphoreType.DMA((2, 2, levels))
@@ -829,13 +865,15 @@
         in_specs=[
             pl.BlockSpec(memory_space=pl.ANY if name.endswith("_hbm") else pltpu.VMEM) for name in operands
         ],
-        out_specs=[pl.BlockSpec(memory_space=pltpu.VMEM)] * len(outs),
+        out_specs=[
+            pl.BlockSpec(memory_space=pl.ANY if name.endswith("_out") else pltpu.VMEM) for name in outs
+        ],
         scratch_shapes=list(scratch.values()),
         compiler_params=pltpu.CompilerParams(
             collective_id=1, has_side_effects=True, vmem_limit_bytes=60 * 2**20
         ),
     )(*operands.values())
-    features, grad_in, sum_wa, sum_ba, sum_wb, sum_bb = got
+    features, grad_in, sum_wa, sum_ba, sum_wb, sum_bb = landed(got)
     return (
         features.reshape(cotangent.shape),
         jnp.transpose(grad_in.reshape(c1, ny, nz, nx), (0, 3, 1, 2)),

time: 73.9 us -> 69.5 us (0.940)
  local copies, waits for them, and re-layouts: 6.9 us -> 0 us
  Pallas kernels: 66.2 us -> 68.7 us
    unnamed x14 -> x0, local copies, waits for them, and re-layouts: 6.9 us -> none
    pallas_call x0 -> x1, Pallas kernels: none -> 2.82 us  [landed(): pl.pallas_call(functools.partial(landing_kernel, count), out_shape=[jax.S...]
where the time goes in v6:
time: 69.5 us; the launch traced here: 69.4 us
  Pallas kernels  68.7 us (99%)
    pallas_call x1, Pallas kernels, on_device(): pl.pallas_call(functools.partial(whole_kernel, (fine_size, coarse_size, (...  65.9 us
    pallas_call x1, Pallas kernels, landed(): pl.pallas_call(functools.partial(landing_kernel, count), out_shape=[jax.S...  2.82 us

profile of v6, /device:TPU:1, one launch (start us, length us, event | category | flops | bytes accessed | tf_op | source)
XLA Modules:
  0.0 69.4 jit_solution(7860835189941887345)
XLA Ops:
  0.6 65.9 %shard_map.109 = (bf16[128,4,128]{2,1,0:T(4,128)(2,1)}, bf16[32,128,32]{2,1,0:T(8,128)(2,1)}, f32[864,64]{1,0:T(8,128)}, f32[1,64]{1,0:T(1,128)}, f32[1728,128]{1,0:T(8,128)}, /*index=5*/f32[1,128]{1,0:T(1,128)}) custom-call(bf16[32,128,32]{2,1,0:T(8,128)(2,1)} %bitcast.18, bf16[864,64]{1,0:T(8,128)(2,1)} %bitcast.20, f32[1,64]{1,0:T(1,128)} %bitcast.22, ...), custom_call_target="tpu_custom_call" | custom-call | tf_op jit(solution)/shard_map/pallas_call | solution.py:862
  66.6 2.8 %shard_map.110 = (bf16[128,4,128]{2,1,0:T(4,128)(2,1)}, bf16[32,128,32]{2,1,0:T(8,128)(2,1)}, f32[864,64]{1,0:T(8,128)}, f32[1,64]{1,0:T(1,128)}, f32[1728,128]{1,0:T(8,128)}, /*index=5*/f32[1,128]{1,0:T(1,128)}) custom-call(bf16[128,4,128]{2,1,0:T(4,128)(2,1)} %get-tuple-element.18.refs_0_, bf16[32,128,32]{2,1,0:T(8,128)(2,1)} %get-tuple-element.19.refs_1_, ...), custom_call_target="tpu_custom_call" | custom-call | tf_op jit(solution)/shard_map/pallas_call | solution.py:772

commit v7 on v6

--- a/solution.py
+++ b/solution.py
@@ -634,12 +634,9 @@
 
     loads["w_a"].wait()
     loads["w_b"].wait()
-    taps = 9
-    for dx in range(3):
-        out_a[dx] = w_a[dx * taps * c1 : (dx + 1) * taps * c1].T
-        for k in range(taps):
-            tap = 26 - dx * taps - k
-            in_a[dx, :, k * c2 : (k + 1) * c2] = w_a[tap * c1 : (tap + 1) * c1]
+    out_a[...] = w_a[...].T
+    for k in range(27):
+        in_a[:, k * c2 : (k + 1) * c2] = w_a[(26 - k) * c1 : (27 - k) * c1]
     out_b[...] = w_b[...].T
     for k in range(27):
         in_b[:, k * c3 : (k + 1) * c3] = w_b[(26 - k) * c2 : (27 - k) * c2]
@@ -657,9 +654,8 @@
     many = 2 * coarse.fold
 
     def forward_a(g, carry):
-        before = bias_a
-        for dx in range(3):
-            before = before + dot(out_a[dx], win_a[:, lanes_at(g * many + dx, many)])
+        near = [win_a[:, lanes_at(g * many + dx, many)] for dx in range(3)]
+        before = dot(out_a[...], jnp.concatenate(near, axis=0)) + bias_a
         before_a[:, lanes_at(g * many, many)] = before
         active = before * jax.nn.sigmoid(before)
         pieces = []
@@ -682,13 +678,13 @@
     grad_b[...] = (mixed[...].astype(jnp.float32) * slope_of(before)).astype(bf16)
     halos["gb"].pack(grad_b)
     halos["gb"].start()
-    feat[...] = (before * jax.nn.sigmoid(before)).astype(bf16)
-    feats.pack(feat)
     top_b = out_wb.shape[0]
     grad = grad_b[...]
     acc_b[:top_b] = dot_rows(win_b[...], grad)
     acc_b[top_b : top_b + 8] = dot_rows(jnp.ones((8, grad.shape[1]), bf16), grad)
     sum_b.start()
+    feat[...] = (before * jax.nn.sigmoid(before)).astype(bf16)
+    feats.pack(feat)
     halos["gb"].wait()
     halos["gb"].coarse_windows(grad_b, strips["gb"], win_gb)
     pooled[...] = dot(in_b[...], win_gb[...]).astype(bf16)
@@ -704,7 +700,6 @@
 
     lax.fori_loop(0, coarse.tiles, backward_b, 0)
     halos["ga"].pack(grad_a)
-    halos["ga"].start()
     sum_b.middle()
     grad = grad_a[...]
     half, width = out_wa.shape[0] // 2, out_wa.shape[1]
@@ -714,6 +709,7 @@
     acc_a[:half, width:] = whole[half:]
     acc_a[half : half + 8, :width] = dot_rows(jnp.ones((8, grad.shape[1]), bf16), grad)
     sum_a.start()
+    halos["ga"].start()
     sum_b.between()
     halos["ga"].wait()
     sum_b.last()
@@ -721,9 +717,8 @@
     halos["ga"].fine_windows(grad_a, strips["ga"], win_ga)
 
     def backward_a(g, carry):
-        total = dot(in_a[0], win_ga[:, lanes_at(g * many, many)])
-        for dx in (1, 2):
-            total = total + dot(in_a[dx], win_ga[:, lanes_at(g * many + dx, many)])
+        near = [win_ga[:, lanes_at(g * many + dx, many)] for dx in range(3)]
+        total = dot(in_a[...], jnp.concatenate(near, axis=0))
         for i in range(many):
             tile = total[:, i * LANES : (i + 1) * LANES].astype(bf16).astype(jnp.float32)
             rows_out[pl.ds(g * many + i, c1, stride=PITCH), :] = tile
@@ -843,8 +838,8 @@
             scratch[f"sum_{name}{i}"] = pltpu.VMEM((*shape, LANES), bf16)
     for name in ("cot_sent", "cot_came", "feat_sent", "feat_came"):
         scratch[name] = pltpu.VMEM((levels, c3 // coarse.fold, LANES), bf16)
-    local["to_a"] = pltpu.VMEM((3, c2, 9 * c1), bf16)
-    local["from_a"] = pltpu.VMEM((3, c1, 9 * c2), bf16)
+    local["to_a"] = pltpu.VMEM((c2, 27 * c1), bf16)
+    local["from_a"] = pltpu.VMEM((c1, 27 * c2), bf16)
     local["to_b"] = pltpu.VMEM((c3, 27 * c2), bf16)
     local["from_b"] = pltpu.VMEM((c2, 27 * c3), bf16)
     local["spread"] = pltpu.VMEM((LANES, coarse.fold * LANES), bf16)

time: 69.5 us -> 69.5 us (level)
  no operation moved by 1% of the time
where the time goes in v7:
time: 69.5 us; the launch traced here: 69.4 us
  Pallas kernels  68.6 us (99%)
  between operations  0.8 us (1%)
    pallas_call x1, Pallas kernels, on_device(): pl.pallas_call(functools.partial(whole_kernel, (fine_size, coarse_size, (...  65.8 us
    pallas_call x1, Pallas kernels, landed(): pl.pallas_call(functools.partial(landing_kernel, count), out_shape=[jax.S...  2.82 us

profile of v7, /device:TPU:1, one launch (start us, length us, event | category | flops | bytes accessed | tf_op | source)
XLA Modules:
  0.0 69.4 jit_solution(8945913688666884768)
XLA Ops:
  0.6 65.8 %shard_map.109 = (bf16[128,4,128]{2,1,0:T(4,128)(2,1)}, bf16[32,128,32]{2,1,0:T(8,128)(2,1)}, f32[864,64]{1,0:T(8,128)}, f32[1,64]{1,0:T(1,128)}, f32[1728,128]{1,0:T(8,128)}, /*index=5*/f32[1,128]{1,0:T(1,128)}) custom-call(bf16[32,128,32]{2,1,0:T(8,128)(2,1)} %bitcast.18, bf16[864,64]{1,0:T(8,128)(2,1)} %bitcast.20, f32[1,64]{1,0:T(1,128)} %bitcast.22, ...), custom_call_target="tpu_custom_call" | custom-call | tf_op jit(solution)/shard_map/pallas_call | solution.py:857
  66.4 2.8 %shard_map.110 = (bf16[128,4,128]{2,1,0:T(4,128)(2,1)}, bf16[32,128,32]{2,1,0:T(8,128)(2,1)}, f32[864,64]{1,0:T(8,128)}, f32[1,64]{1,0:T(1,128)}, f32[1728,128]{1,0:T(8,128)}, /*index=5*/f32[1,128]{1,0:T(1,128)}) custom-call(bf16[128,4,128]{2,1,0:T(4,128)(2,1)} %get-tuple-element.18.refs_0_, bf16[32,128,32]{2,1,0:T(8,128)(2,1)} %get-tuple-element.19.refs_1_, ...), custom_call_target="tpu_custom_call" | custom-call | tf_op jit(solution)/shard_map/pallas_call | solution.py:767
